TPU v7x, 32 devices: a whole 2x2x4 slice. The times are simulated.
32 devices in a mesh: rep: 2 (over x), lev: 4 (over z), tile: 4 (over y, core).
Axes of the slice: x: 2, y: 2, z: 4, core: 2. Of those that a mesh axis runs over, the one named last changes fastest.
Arguments:
- tokens: bfloat16 [2, 8, 4, 8, 8, 768], P('rep', 'lev', 'tile'), may hold values from -6 to 6
- w_qkv: bfloat16 [768, 2304], P('tile'), may hold values from -0.21875 to 0.21875
- w_proj: bfloat16 [768, 768], P('tile'), may hold values from -0.21875 to 0.21875
- seam_codes: int32 [4, 2], replicated, may hold values from 0 to 1
- upstream: bfloat16 [2, 8, 4, 8, 8, 768], P('rep', 'lev', 'tile'), may hold values from -6 to 6
Outputs:
- output: bfloat16 [2, 8, 4, 8, 8, 768], P('rep', 'lev', 'tile')
- grad_tokens: bfloat16 [2, 8, 4, 8, 8, 768], P('rep', 'lev', 'tile')
- grad_qkv: float32 [768, 2304], P('tile')
- grad_proj: float32 [768, 768], P('tile')
Inputs may be any that keep to these rules, and one draw needn't show every extreme that they name: The tiles form a periodic grid of four rows of 1 tiles: tile t's eastern neighbour is (t + 1) mod 4 and its northern neighbour (t + 1) mod 4. seam_codes[t, 0] is 1 where the seam to the eastern neighbour runs reversed, seam_codes[t, 1] likewise for the northern neighbour.
All inputs are finite; a program needn't handle non-finite values.
Results may differ from a plain program's by a relative error of at most 0.019.
Values may be sent and summed in bfloat16 or wider, within the bound.
No kernel may reach another device: no remote copies, remote signals or barrier semaphores. Data moves between devices by JAX's collectives and lax.ppermute only.
A program may use at most 64 MiB of HBM per device.

v0:
```python
import jax
import jax.numpy as jnp
from jax import lax
from jax.experimental import pallas as pl
from jax.experimental.pallas import tpu as pltpu
from jax.sharding import PartitionSpec as P

HEAD_DIM = 32
WIN = 8
WIN_LEV = 2


EPSILON = 1e-05


def shifted(value, axis, steps):
    count = lax.axis_size(axis)
    pairs = [(source, (source + steps) % count) for source in range(count)]
    return lax.ppermute(value, axis, pairs)


def layer_stats(token_rows):
    values = token_rows.astype(jnp.float32)
    center = jnp.mean(values, axis=1, keepdims=True)
    spread = jnp.mean(jnp.square(values - center), axis=1, keepdims=True)
    inverse = lax.rsqrt(spread + EPSILON)
    return ((values - center) * inverse, inverse)


def norm_backward(upstream_rows, grad_hidden, normalized, inverse):
    centre = jnp.mean(grad_hidden, axis=1, keepdims=True)
    projected = jnp.mean(grad_hidden * normalized, axis=1, keepdims=True)
    total_grad = (
        upstream_rows.astype(jnp.float32)
        + (grad_hidden - centre - normalized * projected) * inverse
    )
    return total_grad.astype(jnp.bfloat16)


def roll_local(grid_field, east_flag, north_flag, north_step):
    shift_cells = WIN // 2
    east_part = shifted(grid_field[:, :, :shift_cells], "tile", -1)
    east_part = jnp.where(east_flag, east_part[:, ::-1], east_part)
    across = jnp.concatenate([grid_field[:, :, shift_cells:], east_part], axis=2)
    north_part = shifted(across[:, :shift_cells], "tile", -north_step)
    north_part = jnp.where(north_flag, north_part[:, :, ::-1], north_part)
    upward = jnp.concatenate([across[:, shift_cells:], north_part], axis=1)
    level_part = shifted(upward[:1], "lev", -1)
    return jnp.concatenate([upward[1:], level_part], axis=0)


def unroll_local(rolled, east_flag, north_flag, north_step):
    shift_cells = WIN // 2
    extent = rolled.shape[1]
    level_part = shifted(rolled[-1:], "lev", 1)
    upward = jnp.concatenate([level_part, rolled[:-1]], axis=0)
    north_part = upward[:, extent - shift_cells :]
    north_part = jnp.where(north_flag, north_part[:, :, ::-1], north_part)
    north_part = shifted(north_part, "tile", north_step)
    across = jnp.concatenate([north_part, upward[:, : extent - shift_cells]], axis=1)
    east_part = across[:, :, extent - shift_cells :]
    east_part = jnp.where(east_flag, east_part[:, ::-1], east_part)
    east_part = shifted(east_part, "tile", 1)
    return jnp.concatenate([east_part, across[:, :, : extent - shift_cells]], axis=2)


def to_windows(grid_field):
    levels = grid_field.shape[0]
    extent = grid_field.shape[1]
    channels = grid_field.shape[3]
    blocks = grid_field.reshape(
        levels // WIN_LEV, WIN_LEV, extent // WIN, WIN, extent // WIN, WIN, channels
    )
    blocks = blocks.transpose(0, 2, 4, 1, 3, 5, 6)
    return blocks.reshape(-1, WIN_LEV * WIN * WIN, channels)


def from_windows(windows, levels, extent):
    channels = windows.shape[-1]
    blocks = windows.reshape(
        levels // WIN_LEV, extent // WIN, extent // WIN, WIN_LEV, WIN, WIN, channels
    )
    blocks = blocks.transpose(0, 3, 1, 4, 2, 5, 6)
    return blocks.reshape(levels, extent, extent, channels)


def split_heads(packed):
    windows = packed.shape[0]
    tokens = packed.shape[1]
    model_width = packed.shape[2] // 3
    head_count = model_width // HEAD_DIM
    query_part = packed[:, :, :model_width].reshape(windows, tokens, head_count, HEAD_DIM)
    key_part = packed[:, :, model_width : 2 * model_width].reshape(
        windows, tokens, head_count, HEAD_DIM
    )
    value_part = packed[:, :, 2 * model_width :].reshape(windows, tokens, head_count, HEAD_DIM)
    return (query_part, key_part, value_part)


def window_mask(wrap_flags, tokens):
    level_of = jnp.arange(tokens, dtype=jnp.int32) // (WIN * WIN)
    same_level = level_of[:, None] == level_of[None, :]
    allowed = jnp.logical_or(
        same_level[None, None], jnp.logical_not(wrap_flags)[:, None, None, None]
    )
    return allowed.astype(jnp.float32)


def attend_forward(packed, wrap_flags):
    query_part, key_part, value_part = split_heads(packed)
    scores = jnp.einsum(
        "wqhd,wkhd->whqk", query_part, key_part, preferred_element_type=jnp.float32
    ) * HEAD_DIM ** (-0.5)
    raised = jnp.exp(scores) * window_mask(wrap_flags, packed.shape[1])
    prob = raised / jnp.sum(raised, axis=-1, keepdims=True)
    prob_low = prob.astype(jnp.bfloat16)
    attended = jnp.einsum(
        "whqk,wkhd->wqhd", prob_low, value_part, preferred_element_type=jnp.float32
    )
    attended = attended.astype(jnp.bfloat16).reshape(packed.shape[0], packed.shape[1], -1)
    return (attended, prob, prob_low)


def attend_backward(packed, back_windows, prob, prob_low):
    query_part, key_part, value_part = split_heads(packed)
    back_heads = back_windows.reshape(query_part.shape)
    grad_value = jnp.einsum(
        "whqk,wqhd->wkhd", prob_low, back_heads, preferred_element_type=jnp.float32
    )
    grad_prob = jnp.einsum(
        "wqhd,wkhd->whqk", back_heads, value_part, preferred_element_type=jnp.float32
    )
    centre = jnp.sum(prob * grad_prob, axis=-1, keepdims=True)
    grad_scores = (prob * (grad_prob - centre) * HEAD_DIM ** (-0.5)).astype(jnp.bfloat16)
    grad_query = jnp.einsum(
        "whqk,wkhd->wqhd", grad_scores, key_part, preferred_element_type=jnp.float32
    )
    grad_key = jnp.einsum(
        "whqk,wqhd->wkhd", grad_scores, query_part, preferred_element_type=jnp.float32
    )
    windows = packed.shape[0]
    tokens = packed.shape[1]
    joined = jnp.concatenate(
        [
            grad_query.reshape(windows, tokens, -1),
            grad_key.reshape(windows, tokens, -1),
            grad_value.reshape(windows, tokens, -1),
        ],
        axis=-1,
    )
    return joined.astype(jnp.bfloat16)


def shards_general(tokens, w_qkv, w_proj, seam_codes, upstream):
    levels = tokens.shape[1]
    extent = tokens.shape[3]
    model_width = tokens.shape[5]
    tiles_count = lax.axis_size("tile")
    north_step = tiles_count // 4
    tile_here = lax.axis_index("tile")
    east_flag = seam_codes[tile_here, 0] == 1
    north_flag = seam_codes[tile_here, 1] == 1
    top_level = lax.axis_index("lev") == lax.axis_size("lev") - 1
    per_level = extent // WIN * (extent // WIN)
    window_total = levels // WIN_LEV * per_level
    lev_window = jnp.arange(window_total, dtype=jnp.int32) // per_level
    wrap_flags = jnp.logical_and(top_level, lev_window == levels // WIN_LEV - 1)
    contract_last = (((1,), (1,)), ((), ()))
    contract_first = (((0,), (0,)), ((), ()))
    grid_in = tokens.reshape(levels, extent, extent, model_width)
    grid_up = upstream.reshape(levels, extent, extent, model_width)
    paired = roll_local(
        jnp.concatenate([grid_in, grid_up], axis=-1), east_flag, north_flag, north_step
    )
    grid_in = paired[..., :model_width]
    grid_up = paired[..., model_width:]
    token_rows = grid_in.reshape(-1, model_width)
    upstream_rows = grid_up.reshape(-1, model_width)
    normalized, inverse = layer_stats(token_rows)
    hidden = normalized.astype(jnp.bfloat16)
    full_qkv, full_proj = (
        lax.all_gather(w_qkv, "tile", axis=0, tiled=True),
        lax.all_gather(w_proj, "tile", axis=0, tiled=True),
    )
    projected = jnp.dot(hidden, full_qkv, preferred_element_type=jnp.float32).astype(jnp.bfloat16)
    grid_qkv = projected.reshape(levels, extent, extent, 3 * model_width)
    windows_qkv = to_windows(grid_qkv)
    attended, prob, prob_low = attend_forward(windows_qkv, wrap_flags)
    grid_mixed = from_windows(attended, levels, extent)
    mixed_in = grid_mixed.reshape(-1, model_width)
    mixed_out = lax.dot_general(
        mixed_in, full_proj, contract_last, preferred_element_type=jnp.float32
    )
    back_mix = jnp.dot(upstream_rows, full_proj, preferred_element_type=jnp.float32)
    output_low = (token_rows.astype(jnp.float32) + mixed_out).astype(jnp.bfloat16)
    back_low = back_mix.astype(jnp.bfloat16)
    grid_back = back_low.reshape(levels, extent, extent, model_width)
    grad_windows = attend_backward(windows_qkv, to_windows(grid_back), prob, prob_low)
    grid_grad = from_windows(grad_windows, levels, extent)
    grad_qkv_tok = grid_grad.reshape(-1, 3 * model_width)
    grad_hidden = lax.dot_general(
        grad_qkv_tok, full_qkv, contract_last, preferred_element_type=jnp.float32
    )
    grad_low = norm_backward(upstream_rows, grad_hidden, normalized, inverse)
    grid_output = output_low.reshape(levels, extent, extent, model_width)
    grid_dx = grad_low.reshape(levels, extent, extent, model_width)
    paired = unroll_local(
        jnp.concatenate([grid_output, grid_dx], axis=-1), east_flag, north_flag, north_step
    )
    grid_output = paired[..., :model_width]
    grid_dx = paired[..., model_width:]
    columns = hidden
    share_qkv = lax.psum_scatter(
        lax.dot_general(
            columns, grad_qkv_tok, contract_first, preferred_element_type=jnp.float32
        ).astype(jnp.bfloat16),
        "tile",
        scatter_dimension=0,
        tiled=True,
    )
    columns = upstream_rows
    share_proj = lax.psum_scatter(
        lax.dot_general(
            columns, mixed_in, contract_first, preferred_element_type=jnp.float32
        ).astype(jnp.bfloat16),
        "tile",
        scatter_dimension=0,
        tiled=True,
    )
    grad_qkv, grad_proj = (
        lax.psum(share_qkv, ("rep", "lev")).astype(jnp.float32),
        lax.psum(share_proj, ("rep", "lev")).astype(jnp.float32),
    )
    return (grid_output.reshape(tokens.shape), grid_dx.reshape(tokens.shape), grad_qkv, grad_proj)


LANES = 128
MAIN_MEBIBYTES = 56
NEAR = LANES // HEAD_DIM


def swapped(value, axis, mask):
    count = lax.axis_size(axis)
    return lax.ppermute(value, axis, [(source, source ^ mask) for source in range(count)])


def roll_source(codes_ref, cell, tile_here, tiles_count, extent):
    half = WIN // 2
    north_step = tiles_count // 4
    slot = cell // (extent * extent)
    row = (cell // extent) % extent
    col = cell % extent

    def code_of(tile, which):
        found = jnp.zeros_like(tile)
        for t in range(tiles_count):
            found = jnp.where(tile == t, codes_ref[t, which], found)
        return found == 1

    tile = jnp.bitwise_xor(slot, tile_here)
    crossed = row >= extent - half
    col1 = jnp.where(crossed & code_of(tile, 1), extent - 1 - col, col)
    row1 = jnp.where(crossed, row - (extent - half), row + half)
    tile1 = jnp.where(crossed, (tile + north_step) % tiles_count, tile)
    crossed = col1 >= extent - half
    row2 = jnp.where(crossed & code_of(tile1, 0), extent - 1 - row1, row1)
    col2 = jnp.where(crossed, col1 - (extent - half), col1 + half)
    tile2 = jnp.where(crossed, (tile1 + 1) % tiles_count, tile1)
    return (jnp.bitwise_xor(tile2, tile_here) * extent + row2) * extent + col2


def in_order(slots, here):
    bit = 1
    while bit < len(slots):
        odd = jnp.bitwise_and(here, bit) != 0
        slots = [jnp.where(odd, slots[k ^ bit], slots[k]) for k in range(len(slots))]
        bit *= 2
    return slots


def dot_nn(a, b):
    return lax.dot_general(a, b, (((1,), (0,)), ((), ())), preferred_element_type=jnp.float32)


def dot_nt(a, b):
    return lax.dot_general(a, b, (((1,), (1,)), ((), ())), preferred_element_type=jnp.float32)


def dot_tn(a, b):
    return lax.dot_general(a, b, (((0,), (0,)), ((), ())), preferred_element_type=jnp.float32)


def deal_kernel(scal_ref, qkv_any, out_any, in_any, up_any, high_ref, low_ref, *refs):
    *block_refs, qkv_ref, out_ref, sems = refs
    tiles_count = len(block_refs)
    channels = out_ref.shape[1]
    own = channels // tiles_count
    rep, here = scal_ref[0], scal_ref[1]
    copies = [
        pltpu.make_async_copy(source.at[level], target.at[:, first : first + channels], sems.at[2 * level + which])
        for level, target in ((0, low_ref), (1, high_ref))
        for which, (source, first) in enumerate(((in_any, 0), (up_any, channels)))
    ]
    copies.append(pltpu.make_async_copy(qkv_any, qkv_ref, sems.at[4]))
    copies.append(pltpu.make_async_copy(out_any, out_ref, sems.at[5]))
    for copy in copies:
        copy.start()
    for copy in copies:
        copy.wait()

    def columns(which, tile):
        ref = out_ref if which == 3 else qkv_ref
        base = (0 if which == 3 else which * channels) + tile * own
        return ref[:, base : base + LANES], ref[:, base + LANES : base + own]

    blocks = []
    for tile in range(tiles_count):
        (q, q1), (k, k1), (v, v1), (p, p1) = [columns(which, tile) for which in range(4)]
        blocks.append(jnp.concatenate([q, k, q1, k1, v, p, v1, p1], axis=1))
    for slot, (ref, block) in enumerate(zip(block_refs, in_order(blocks, here))):
        if slot >= 2:
            half = block.shape[0] // 2
            block = jnp.where(rep == 0, block[:half], block[half:])
        ref[...] = block


def attend_window(block, allowed):
    tokens = block.shape[0]
    lane = lax.broadcasted_iota(jnp.int32, (1, LANES), 1)
    group = [block[:, g * LANES : (g + 1) * LANES] for g in range(6)]
    scale = HEAD_DIM ** (-0.5)

    def turned(x):
        return pltpu.roll(x.astype(jnp.float32), LANES // 2, 1)

    def attend(q, k, v, o, heads):
        masks = [lane // HEAD_DIM == h for h in range(heads)]

        def stacked(x):
            return jnp.concatenate([jnp.where(m, x, jnp.zeros_like(x)) for m in masks], axis=0)

        def folded(x):
            total = jnp.where(masks[0], x[:tokens], 0.0)
            for h in range(1, heads):
                total = jnp.where(masks[h], x[h * tokens : (h + 1) * tokens], total)
            return total

        k_all, v_all = stacked(k), stacked(v)
        scores = (dot_nt(k_all, q) * scale).reshape(heads, tokens, tokens)
        raised = jnp.exp(scores) * allowed[None]
        prob = raised / jnp.sum(raised, axis=1, keepdims=True)
        grad_prob = dot_nt(v_all, o).reshape(heads, tokens, tokens)
        centre = jnp.sum(prob * grad_prob, axis=1, keepdims=True)
        grad_scores = (prob * (grad_prob - centre) * scale).astype(jnp.bfloat16).reshape(-1, tokens)
        prob_low = prob.astype(jnp.bfloat16).reshape(-1, tokens)
        att = dot_tn(prob_low, v_all)
        grad_q = dot_tn(grad_scores, k_all)
        grad_k = folded(dot_nn(grad_scores, q))
        grad_v = folded(dot_nn(prob_low, o))
        return grad_q, grad_k, grad_v, att

    gq, gk, gv, att = attend(group[0], group[1], group[3], group[4], NEAR)
    qk_turned = turned(group[2]).astype(jnp.bfloat16)
    vo_turned = turned(group[5]).astype(jnp.bfloat16)
    gq1, gk1, gv1, att1 = attend(group[2], qk_turned, group[5], vo_turned, NEAR // 2)
    parts = [gq, gk, gq1 + turned(gk1), gv, att, gv1 + turned(att1)]
    return jnp.concatenate(parts, axis=1).astype(jnp.bfloat16)


def main_kernel(scal_ref, codes_ref, *refs):
    *refs, inner_ref, outer_ref, wts, keep_a, send_a, keep_b, send_b, hid, up, rolled, result, fields, sems = refs
    tiles_count = (len(refs) + 2) // 4
    cells_refs = refs[: 2 * tiles_count]
    near_refs = refs[2 * tiles_count : 2 * tiles_count + 2]
    far_refs = refs[2 * tiles_count + 2 :]
    cells = cells_refs[0].shape[0]
    channels = wts.shape[0]
    rows = channels // tiles_count
    half = rows // 2
    plane = tiles_count * cells
    wrapped, rep, here = scal_ref[0], scal_ref[1], scal_ref[2]
    copies = []

    def fetch(source, target):
        copy = pltpu.make_async_copy(source, target, sems.at[len(copies)])
        copy.start()
        copies.append(copy)

    for k in range(tiles_count):
        for l in range(2):
            fetch(cells_refs[2 * k + l], fields.at[pl.ds(l * plane + k * cells, cells)])
    for k in range(tiles_count):
        base = (here ^ k) * rows
        if k < 2:
            fetch(near_refs[k], wts.at[pl.ds(pl.multiple_of(base, 32), rows)])
        else:
            fetch(far_refs[2 * k - 4], wts.at[pl.ds(pl.multiple_of(base + rep * half, 32), half)])
            fetch(far_refs[2 * k - 3], wts.at[pl.ds(pl.multiple_of(base + (1 - rep) * half, 32), half)])
    for copy in copies[: 2 * tiles_count]:
        copy.wait()
    for at in range(0, 2 * plane, cells):
        x = fields[at : at + cells, :channels].astype(jnp.float32)
        center = jnp.mean(x, axis=1, keepdims=True)
        x = x - center
        spread = jnp.mean(jnp.square(x), axis=1, keepdims=True)
        hid[at : at + cells, :] = (x * lax.rsqrt(spread + EPSILON)).astype(jnp.bfloat16)
        up[at : at + cells, :] = fields[at : at + cells, channels:]
    for copy in copies[2 * tiles_count :]:
        copy.wait()

    lane = lax.broadcasted_iota(jnp.int32, (1, LANES), 1)
    low = lane < LANES // 2
    split = 4 * LANES
    extent = WIN
    source = roll_source(codes_ref, lax.broadcasted_iota(jnp.int32, (plane, 1), 0), here, tiles_count, extent)
    from_col = lax.broadcasted_iota(jnp.int32, (plane, plane), 1) == source
    selector = jnp.where(from_col, 1.0, 0.0).astype(jnp.bfloat16)
    source = roll_source(codes_ref, lax.broadcasted_iota(jnp.int32, (1, plane), 1), here, tiles_count, extent)
    from_row = lax.broadcasted_iota(jnp.int32, (plane, plane), 0) == source
    back_selector = jnp.where(from_row, 1.0, 0.0).astype(jnp.bfloat16)
    for l in range(2):
        at = slice(l * plane, (l + 1) * plane)
        front = dot_nn(hid[at, :], wts[:, :split])
        last = dot_nn(hid[at, :], wts[:, split + LANES :])
        back = dot_nn(up[at, :], wts[:, split:])
        mixed = jnp.where(low, last, back[:, LANES:])
        whole = jnp.concatenate([front, back[:, :LANES], mixed], axis=1).astype(jnp.bfloat16)
        rolled[l] = dot_nn(selector, whole).astype(jnp.bfloat16)

    tokens = 2 * cells
    level_k = lax.broadcasted_iota(jnp.int32, (tokens, tokens), 0) // cells
    level_q = lax.broadcasted_iota(jnp.int32, (tokens, tokens), 1) // cells
    allowed = jnp.where((level_k == level_q) | (wrapped == 0), 1.0, 0.0)

    def window(w, carry):
        at = pl.ds(pl.multiple_of(w * cells, cells), cells)
        block = jnp.concatenate([rolled[0, at, :], rolled[1, at, :]], axis=0)
        out = attend_window(block, allowed)
        result[0, at, :] = out[:cells]
        result[1, at, :] = out[cells:]
        return carry

    lax.fori_loop(0, tiles_count, window, 0)

    zero = jnp.zeros((plane, LANES), jnp.bfloat16)
    for l in range(2):
        at = slice(l * plane, (l + 1) * plane)
        tok = dot_nn(back_selector, result[l]).astype(jnp.bfloat16)
        tail = tok[:, split + LANES :]
        inner_ref[at, :] = jnp.concatenate([tok[:, :split], zero, jnp.where(low, tail, zero)], axis=1)
        outer_ref[at, :] = jnp.concatenate([tok[:, split : split + LANES], jnp.where(low, zero, tail)], axis=1)
    inner, outer = inner_ref[...], outer_ref[...]
    hid_t = hid[...].T
    up_t = up[...].T
    width = 3 * LANES
    share_b = dot_nn(hid_t, inner[:, width:])
    share_b = jnp.concatenate(
        [share_b[:, :LANES], share_b[:, LANES:] + dot_nn(up_t, outer)], axis=1
    ).astype(jnp.bfloat16)
    share_a = dot_nn(hid_t, inner[:, :width]).astype(jnp.bfloat16)
    for share, keep, send in ((share_b, keep_b, send_b), (share_a, keep_a, send_a)):
        for j in range(tiles_count):
            first = share[j * rows : j * rows + half]
            second = share[j * rows + half : (j + 1) * rows]
            keep[j] = jnp.where(rep == 0, first, second)
            send[j] = jnp.where(rep == 0, second, first)


def rows_kernel(inner_ref, outer_ref, wts, keep_ref, send_ref):
    slots, levels, cells, width = keep_ref.shape
    channels = width // 2
    plane = 2 * slots * cells
    split = 4 * LANES
    for l in range(levels):
        at = slice(l * plane, (l + 1) * plane)
        grad_hidden = dot_nt(inner_ref[at, :], wts[...]).astype(jnp.bfloat16)
        mixed_out = dot_nt(outer_ref[at, :], wts[:, split:]).astype(jnp.bfloat16)
        for k in range(2 * slots):
            ref = send_ref if k % 2 else keep_ref
            at = slice(k * cells, (k + 1) * cells)
            ref[k // 2, l, :, :channels] = mixed_out[at]
            ref[k // 2, l, :, channels:] = grad_hidden[at]


def column_kernel(here_ref, *refs):
    *slot_refs, out_ref = refs
    here = here_ref[0]
    blocks = in_order([ref[...] for ref in slot_refs], here)
    pieces = []
    for which in range(2):
        for block in blocks:
            pieces.append(block[:, which * LANES : (which + 1) * LANES])
            rest = 2 * LANES + which * (LANES // 2)
            pieces.append(block[:, rest : rest + LANES // 2])
    out_ref[...] = jnp.concatenate(pieces, axis=1)


SMEM_SPEC = pl.BlockSpec(memory_space=pltpu.SMEM)
VMEM_SPEC = pl.BlockSpec(memory_space=pltpu.VMEM)
ANY_SPEC = pl.BlockSpec(memory_space=pl.ANY)


def call(body, outs, scalars, arrays, flops, mebibytes, scratch=(), spec=VMEM_SPEC):
    moved = sum(a.size * a.dtype.itemsize for a in arrays) + sum(o.size * o.dtype.itemsize for o in outs)
    return pl.pallas_call(
        body,
        out_shape=outs,
        in_specs=[SMEM_SPEC] * len(scalars) + [spec] * len(arrays),
        out_specs=[VMEM_SPEC] * len(outs),
        scratch_shapes=list(scratch),
        compiler_params=pltpu.CompilerParams(vmem_limit_bytes=mebibytes * 1024 * 1024),
        cost_estimate=pl.CostEstimate(flops=flops, bytes_accessed=moved, transcendentals=0),
    )(*scalars, *arrays)


def low_shape(*shape):
    return jax.ShapeDtypeStruct(shape, jnp.bfloat16)


def added(a, b):
    return (a.astype(jnp.float32) + b.astype(jnp.float32)).astype(jnp.bfloat16)


def parted(value, dim, bit):
    size = value.shape[dim] // 2
    keep = lax.dynamic_slice_in_dim(value, bit * size, size, dim)
    send = lax.dynamic_slice_in_dim(value, (1 - bit) * size, size, dim)
    return keep, send


def joined(mine, other, bit, dim=0):
    odd = bit == 1
    return jnp.concatenate([jnp.where(odd, other, mine), jnp.where(odd, mine, other)], axis=dim)


def bits_of(count):
    bits, bit = [], 1
    while bit < count:
        bits.append(bit)
        bit *= 2
    return bits


def reduce_share(keep, send, lev_here, tile_here):
    came = swapped(send, "rep", 1)
    part = added(keep, came)
    for bit in bits_of(lax.axis_size("lev")):
        keep, send = parted(part, 1, (lev_here // bit) % 2)
        came = swapped(send, "lev", bit)
        part = added(keep, came)
    tiles_count = lax.axis_size("tile")
    near = tile_here % 2
    pairs = part.reshape(tiles_count // 2, 2, *part.shape[1:])
    mine = lax.dynamic_index_in_dim(pairs, near, 1, keepdims=False)
    away = lax.dynamic_index_in_dim(pairs, 1 - near, 1, keepdims=False)
    came = swapped(away, "tile", 1)
    both = jnp.stack([mine, came], axis=1)
    far = tile_here // 2
    slots = lax.dynamic_index_in_dim(both, far, 0, keepdims=False)
    found = [slots[0], slots[1]]
    for mask in range(1, tiles_count // 2):
        got = swapped(lax.dynamic_index_in_dim(both, far ^ mask, 0, keepdims=False), "tile", 2 * mask)
        found += [got[0], got[1]]
    rows, cols = part.shape[1:]
    channels = tiles_count * cols // 2
    here = tile_here.reshape(1).astype(jnp.int32)
    return call(column_kernel, [low_shape(rows, 2 * channels)], [here], found, 1000, 4)[0]


def spread(piece, lev_here, rep_here):
    for bit in reversed(bits_of(lax.axis_size("lev"))):
        came = swapped(piece, "lev", bit)
        piece = joined(piece, came, (lev_here // bit) % 2)
    came = swapped(piece, "rep", 1)
    return joined(piece, came, rep_here)


def shards_by_heads(tokens, w_qkv, w_proj, seam_codes, upstream):
    levels, extent, channels = tokens.shape[1], tokens.shape[3], tokens.shape[5]
    cells = extent * extent
    tiles_count = lax.axis_size("tile")
    rep_here, lev_here, tile_here = lax.axis_index("rep"), lax.axis_index("lev"), lax.axis_index("tile")
    shard_rows = w_qkv.shape[0]
    wrapped = lev_here == lax.axis_size("lev") - 1
    field_in = tokens.reshape(levels, cells, channels)
    field_up = upstream.reshape(levels, cells, channels)
    half = shard_rows // 2

    shape = low_shape(cells, 2 * channels)
    high, low, *blocks = call(
        deal_kernel,
        [shape, shape]
        + [low_shape(shard_rows, channels)] * 2
        + [low_shape(half, channels)] * (tiles_count - 2),
        [jnp.stack([rep_here.astype(jnp.int32), tile_here.astype(jnp.int32)])],
        [w_qkv, w_proj, field_in, field_up],
        1000,
        MAIN_MEBIBYTES,
        scratch=[
            pltpu.VMEM(w_qkv.shape, jnp.bfloat16),
            pltpu.VMEM(w_proj.shape, jnp.bfloat16),
            pltpu.SemaphoreType.DMA((6,)),
        ],
        spec=ANY_SPEC,
    )
    low = shifted(low, "lev", -1)
    weights = [blocks[0]]
    for k in range(1, tiles_count):
        weights.append(swapped(blocks[k], "tile", k))
        if k >= 2:
            weights.append(swapped(weights[-1], "rep", 1))

    def gathered(piece):
        have = {0: piece}
        for bit in reversed(bits_of(tiles_count)):
            for k in list(have):
                have[k ^ bit] = swapped(have[k], "tile", bit)
        return [have[k] for k in range(tiles_count)]

    pieces = [p for pair in zip(gathered(high), gathered(low)) for p in pair]
    scalars = jnp.stack([wrapped.astype(jnp.int32), rep_here.astype(jnp.int32), tile_here.astype(jnp.int32)])
    plane = tiles_count * cells
    width = 3 * LANES
    part_shape = low_shape(tiles_count, half, width)
    inner_shape = low_shape(levels * plane, 2 * width)
    outer_shape = low_shape(levels * plane, 2 * LANES)
    weight_shape = low_shape(channels, 2 * width)
    inner, outer, weight, keep_a, send_a, keep_b, send_b = call(
        main_kernel,
        [inner_shape, outer_shape, weight_shape, part_shape, part_shape, part_shape, part_shape],
        [scalars, seam_codes],
        [*pieces, *weights],
        8 * levels * plane * channels * channels,
        MAIN_MEBIBYTES,
        scratch=[
            pltpu.VMEM((levels * plane, channels), jnp.bfloat16),
            pltpu.VMEM((levels * plane, channels), jnp.bfloat16),
            pltpu.VMEM((levels, plane, 2 * width), jnp.bfloat16),
            pltpu.VMEM((levels, plane, 2 * width), jnp.bfloat16),
            pltpu.VMEM((levels * plane, 2 * channels), jnp.bfloat16),
            pltpu.SemaphoreType.DMA((len(pieces) + len(weights),)),
        ],
        spec=ANY_SPEC,
    )
    sums_shape = low_shape(tiles_count // 2, levels, cells, 2 * channels)
    keep, send = call(rows_kernel, [sums_shape, sums_shape], [], [inner, outer, weight], 10**9, 16)

    came = swapped(send, "tile", 1)
    sums = added(keep, came)
    slots = [sums[k] for k in range(tiles_count // 2)]
    for bit in bits_of(tiles_count // 2):
        came = swapped(jnp.stack(slots[1::2]), "tile", 2 * bit)
        slots = [added(slots[2 * k], came[k]) for k in range(len(slots) // 2)]
    final = slots[0]
    low_back = shifted(final[1], "lev", 1)
    final = jnp.stack([low_back, final[0]]).reshape(levels * cells, 2 * channels)
    token_rows = field_in.reshape(-1, channels)
    upstream_rows = field_up.reshape(-1, channels)
    normalized, inverse = layer_stats(token_rows)
    output = (token_rows.astype(jnp.float32) + final[:, :channels].astype(jnp.float32)).astype(jnp.bfloat16)
    grad_tokens = norm_backward(upstream_rows, final[:, channels:].astype(jnp.float32), normalized, inverse)

    grad_b, grad_a = [
        spread(reduce_share(*pair, lev_here, tile_here), lev_here, rep_here).astype(jnp.float32)
        for pair in ((keep_b, send_b), (keep_a, send_a))
    ]
    grad_qkv = jnp.concatenate([grad_a, grad_b[:, :channels]], axis=1)
    grad_proj = grad_b[:, channels:]
    return (output.reshape(tokens.shape), grad_tokens.reshape(tokens.shape), grad_qkv, grad_proj)


def power_of_two(count):
    return count & (count - 1) == 0


def shards(tokens, w_qkv, w_proj, seam_codes, upstream):
    counts = [lax.axis_size(axis) for axis in ("rep", "lev", "tile")]
    tiles_count = counts[2]
    channels = tokens.shape[5]
    one_window = tokens.shape[0] == 1 and tokens.shape[1] == WIN_LEV and tokens.shape[3] == WIN and tokens.shape[2] == 1
    by_heads = (
        one_window
        and all(power_of_two(count) for count in counts)
        and tiles_count % 4 == 0
        and (channels // HEAD_DIM) % tiles_count == 0
        and channels // tiles_count == LANES + LANES // 2
        and counts[0] == 2
        and (channels // tiles_count) % (8 * counts[0] * counts[1]) == 0
    )
    if not by_heads:
        return shards_general(tokens, w_qkv, w_proj, seam_codes, upstream)
    return shards_by_heads(tokens, w_qkv, w_proj, seam_codes, upstream)


def solution(mesh):
    in_specs = (
        P("rep", "lev", "tile", None, None, None),
        P("tile", None),
        P("tile", None),
        P(),
        P("rep", "lev", "tile", None, None, None),
    )
    out_specs = (
        P("rep", "lev", "tile", None, None, None),
        P("rep", "lev", "tile", None, None, None),
        P("tile", None),
        P("tile", None),
    )
    return jax.shard_map(shards, mesh=mesh, in_specs=in_specs, out_specs=out_specs, check_vma=False)
```

profile of v0, /device:TPU:0, one launch (start us, length us, event | category | flops | bytes accessed | tf_op | source)
XLA Modules:
  0.0 117.7 jit_solution(9183048572354869183)
XLA Ops:
  1.3 3.5 %shard_map.84 = (bf16[64,1536]{1,0:T(8,128)(2,1)}, bf16[64,1536]{1,0:T(8,128)(2,1)}, bf16[192,768]{1,0:T(8,128)(2,1)}, bf16[192,768]{1,0:T(8,128)(2,1)}, bf16[96...) custom-call(s32[2]{0:T(128)} %pad_add_fusion.1.scal_ref, bf16[192,2304]{1,0:T(8,128)(2,1)} %qkv_any.1, ...), custom_call_target="tpu_custom_call" | custom-call | flops 1000 | bytes 2850816 | tf_op jit(solution)/shard_map/pallas_call | solution.py:505
  4.7 5.1 %collective-permute-start = (bf16[64,1536]{1,0:T(8,128)(2,1)}, bf16[64,1536]{1,0:T(8,128)(2,1)S(1)}, u32[]{:S(2)}, u32[]{:S(2)}) collective-permute-start(bf16[64,1536]{1,0:T(8,128)(2,1)} %get-tuple-element.20), channel_id=1, source_target_pairs={{0,12},{4,0},{8,4},{12,8},{1,13},{5,1},{9,5},{13,9},{2,14},{6,2},{... | collective-permute-start | bytes 589832 | tf_op jit(solution)/shard_map/ppermute | solution.py:19
  9.9 1.5 %collective-permute-start.8 = (bf16[96,768]{1,0:T(8,128)(2,1)}, bf16[96,768]{1,0:T(8,128)(2,1)S(1)}, u32[]{:S(2)}, u32[]{:S(2)}) collective-permute-start(bf16[96,768]{1,0:T(8,128)(2,1)} %get-tuple-element.23), channel_id=1, source_target_pairs={{0,2},{1,3},{2,0},{3,1},{4,6},{5,7},{6,4},{7,5},{8,10},{9,11},{10,... | collective-permute-start | bytes 442376 | tf_op jit(solution)/shard_map/ppermute | solution.py:244
  12.4 1.9 %collective-permute-done.refs_1_ = bf16[64,1536]{1,0:T(8,128)(2,1)S(1)} collective-permute-done((bf16[64,1536]{1,0:T(8,128)(2,1)}, bf16[64,1536]{1,0:T(8,128)(2,1)S(1)}, u32[]{:S(2)}, u32[]{:S(2)}) %collective-permute-start) | collective-permute-done | bytes 196640 | tf_op jit(solution)/shard_map/ppermute | solution.py:19
  14.3 1.5 %collective-permute-start.4 = (bf16[64,1536]{1,0:T(8,128)(2,1)S(1)}, bf16[64,1536]{1,0:T(8,128)(2,1)S(1)}, u32[]{:S(2)}, u32[]{:S(2)}) collective-permute-start(bf16[64,1536]{1,0:T(8,128)(2,1)S(1)} %collective-permute-done.refs_1_), channel_id=1, source_target_pairs={{0,2},{1,3},{2,0},{3,1},{4,6},{5,7},{6,4},{7,5},{8,10},{9,11},{10,... | collective-permute-start | bytes 589832 | tf_op jit(solution)/shard_map/ppermute | solution.py:244
  16.1 10.2 %collective-permute-done.10.refs_12_ = bf16[96,768]{1,0:T(8,128)(2,1)S(1)} collective-permute-done((bf16[96,768]{1,0:T(8,128)(2,1)}, bf16[96,768]{1,0:T(8,128)(2,1)S(1)}, u32[]{:S(2)}, u32[]{:S(2)}) %collective-permute-start.10) | collective-permute-done | bytes 147488 | tf_op jit(solution)/shard_map/ppermute | solution.py:244
  26.3 1.5 %collective-permute-start.9 = (bf16[96,768]{1,0:T(8,128)(2,1)S(1)}, bf16[96,768]{1,0:T(8,128)(2,1)S(1)}, u32[]{:S(2)}, u32[]{:S(2)}) collective-permute-start(bf16[96,768]{1,0:T(8,128)(2,1)S(1)} %collective-permute-done.8.refs_10_), channel_id=1, source_target_pairs={{0,16},{16,0},{1,17},{17,1},{2,18},{18,2},{3,19},{19,3},{4,20},{20... | collective-permute-start | bytes 442376 | tf_op jit(solution)/shard_map/ppermute | solution.py:244
  30.4 2.6 %collective-permute-done.9.refs_11_ = bf16[96,768]{1,0:T(8,128)(2,1)S(1)} collective-permute-done((bf16[96,768]{1,0:T(8,128)(2,1)S(1)}, bf16[96,768]{1,0:T(8,128)(2,1)S(1)}, u32[]{:S(2)}, u32[]{:S(2)}) %collective-permute-start.9) | collective-permute-done | bytes 147488 | tf_op jit(solution)/shard_map/ppermute | solution.py:244
  33.0 2.7 %collective-permute-done.11.refs_13_ = bf16[96,768]{1,0:T(8,128)(2,1)S(1)} collective-permute-done((bf16[96,768]{1,0:T(8,128)(2,1)S(1)}, bf16[96,768]{1,0:T(8,128)(2,1)S(1)}, u32[]{:S(2)}, u32[]{:S(2)}) %collective-permute-start.11) | collective-permute-done | bytes 147488 | tf_op jit(solution)/shard_map/ppermute | solution.py:244
  36.6 10.2 %shard_map.85 = (bf16[512,768]{1,0:T(8,128)(2,1)}, bf16[512,256]{1,0:T(8,128)(2,1)}, bf16[768,768]{1,0:T(8,128)(2,1)}, bf16[4,96,384]{2,1,0:T(8,128)(2,1)}, bf16...) custom-call(s32[3]{0:T(128)} %pad_add_fusion.scal_ref, s32[4,2]{1,0:T(4,128)} %copy.9.codes_ref, ...), custom_call_target="tpu_custom_call" | custom-call | flops 2415919104 | bytes 6160384 | tf_op jit(solution)/shard_map/pallas_call | solution.py:505
  46.8 1.6 %collective-permute-start.23 = (bf16[4,96,384]{2,1,0:T(8,128)(2,1)}, bf16[4,96,384]{2,1,0:T(8,128)(2,1)S(1)}, u32[]{:S(2)}, u32[]{:S(2)}) collective-permute-start(bf16[4,96,384]{2,1,0:T(8,128)(2,1)} %get-tuple-element.33), channel_id=1, source_target_pairs={{0,16},{16,0},{1,17},{17,1},{2,18},{18,2},{3,19},{19,3},{4,20},{20... | collective-permute-start | bytes 884744 | tf_op jit(solution)/shard_map/ppermute | solution.py:244
  53.6 2.0 %collective-permute-done.23 = bf16[4,96,384]{2,1,0:T(8,128)(2,1)S(1)} collective-permute-done((bf16[4,96,384]{2,1,0:T(8,128)(2,1)}, bf16[4,96,384]{2,1,0:T(8,128)(2,1)S(1)}, u32[]{:S(2)}, u32[]{:S(2)}) %collective-permute-start.23) | collective-permute-done | bytes 294944 | tf_op jit(solution)/shard_map/ppermute | solution.py:244
  55.8 6.6 %collective-permute-done.15 = bf16[4,96,384]{2,1,0:T(8,128)(2,1)S(1)} collective-permute-done((bf16[4,96,384]{2,1,0:T(8,128)(2,1)S(1)}, bf16[4,96,384]{2,1,0:T(8,128)(2,1)S(1)}, u32[]{:S(2)}, u32[]{:S(2)}) %collective-permute-start.15) | collective-permute-done | bytes 294944 | tf_op jit(solution)/shard_map/ppermute | solution.py:244
  63.8 5.7 %collective-permute-done.16 = bf16[4,48,384]{2,1,0:T(8,128)(2,1)S(1)} collective-permute-done((bf16[4,48,384]{2,1,0:T(8,128)(2,1)S(1)}, bf16[4,48,384]{2,1,0:T(8,128)(2,1)S(1)}, u32[]{:S(2)}, u32[]{:S(2)}) %collective-permute-start.16) | collective-permute-done | bytes 147488 | tf_op jit(solution)/shard_map/ppermute | solution.py:244
  69.8 5.1 %collective-permute-done.17 = bf16[4,24,384]{2,1,0:T(8,128)(2,1)S(1)} collective-permute-done((bf16[4,24,384]{2,1,0:T(8,128)(2,1)S(1)}, bf16[4,24,384]{2,1,0:T(8,128)(2,1)S(1)}, u32[]{:S(2)}, u32[]{:S(2)}) %collective-permute-start.17) | collective-permute-done | bytes 73760 | tf_op jit(solution)/shard_map/ppermute | solution.py:244
  77.3 1.8 %collective-permute-done.27 = bf16[2,24,384]{2,1,0:T(8,128)(2,1)S(1)} collective-permute-done((bf16[2,24,384]{2,1,0:T(8,128)(2,1)S(1)}, bf16[2,24,384]{2,1,0:T(8,128)(2,1)S(1)}, u32[]{:S(2)}, u32[]{:S(2)}) %collective-permute-start.27) | collective-permute-done | bytes 36896 | tf_op jit(solution)/shard_map/ppermute | solution.py:244
  80.4 2.0 %collective-permute-start.20 = (bf16[24,1536]{1,0:T(8,128)(2,1)S(1)}, bf16[24,1536]{1,0:T(8,128)(2,1)S(1)}, u32[]{:S(2)}, u32[]{:S(2)}) collective-permute-start(bf16[24,1536]{1,0:T(8,128)(2,1)S(1)} %shard_map.87), channel_id=1, source_target_pairs={{0,8},{4,12},{8,0},{12,4},{1,9},{5,13},{9,1},{13,5},{2,10},{6,14},... | collective-permute-start | bytes 221192 | tf_op jit(solution)/shard_map/ppermute | solution.py:244
  82.4 4.4 %collective-permute-done.28 = bf16[24,1536]{1,0:T(8,128)(2,1)S(1)} collective-permute-done((bf16[24,1536]{1,0:T(8,128)(2,1)S(1)}, bf16[24,1536]{1,0:T(8,128)(2,1)S(1)}, u32[]{:S(2)}, u32[]{:S(2)}) %collective-permute-start.28) | collective-permute-done | bytes 73760 | tf_op jit(solution)/shard_map/ppermute | solution.py:244
  87.7 1.3 %collective-permute-start.21 = (bf16[48,1536]{1,0:T(8,128)(2,1)S(1)}, bf16[48,1536]{1,0:T(8,128)(2,1)S(1)}, u32[]{:S(2)}, u32[]{:S(2)}) collective-permute-start(bf16[48,1536]{1,0:T(8,128)(2,1)S(1)} %pad_maximum_fusion.4), channel_id=1, source_target_pairs={{0,4},{4,0},{8,12},{12,8},{1,5},{5,1},{9,13},{13,9},{2,6},{6,2},{1... | collective-permute-start | bytes 442376 | tf_op jit(solution)/shard_map/ppermute | solution.py:244
  89.2 3.6 %collective-permute-done.29 = bf16[48,1536]{1,0:T(8,128)(2,1)S(1)} collective-permute-done((bf16[48,1536]{1,0:T(8,128)(2,1)S(1)}, bf16[48,1536]{1,0:T(8,128)(2,1)S(1)}, u32[]{:S(2)}, u32[]{:S(2)}) %collective-permute-start.29) | collective-permute-done | bytes 147488 | tf_op jit(solution)/shard_map/ppermute | solution.py:244
  92.9 1.6 %collective-permute-done.21 = bf16[48,1536]{1,0:T(8,128)(2,1)S(1)} collective-permute-done((bf16[48,1536]{1,0:T(8,128)(2,1)S(1)}, bf16[48,1536]{1,0:T(8,128)(2,1)S(1)}, u32[]{:S(2)}, u32[]{:S(2)}) %collective-permute-start.21) | collective-permute-done | bytes 147488 | tf_op jit(solution)/shard_map/ppermute | solution.py:244
  98.1 6.4 %collective-permute-done.30 = bf16[96,1536]{1,0:T(8,128)(2,1)S(1)} collective-permute-done((bf16[96,1536]{1,0:T(8,128)(2,1)S(1)}, bf16[96,1536]{1,0:T(8,128)(2,1)S(1)}, u32[]{:S(2)}, u32[]{:S(2)}) %collective-permute-start.30) | collective-permute-done | bytes 294944 | tf_op jit(solution)/shard_map/ppermute | solution.py:244
  104.7 2.9 %collective-permute-done.22 = bf16[96,1536]{1,0:T(8,128)(2,1)S(1)} collective-permute-done((bf16[96,1536]{1,0:T(8,128)(2,1)S(1)}, bf16[96,1536]{1,0:T(8,128)(2,1)S(1)}, u32[]{:S(2)}, u32[]{:S(2)}) %collective-permute-start.22) | collective-permute-done | bytes 294944 | tf_op jit(solution)/shard_map/ppermute | solution.py:244
  110.9 5.6 %collective-permute-done.14 = bf16[64,1536]{1,0:T(8,128)(2,1)S(1)} collective-permute-done((bf16[64,1536]{1,0:T(8,128)(2,1)S(1)}, bf16[64,1536]{1,0:T(8,128)(2,1)S(1)}, u32[]{:S(2)}, u32[]{:S(2)}) %collective-permute-start.14) | collective-permute-done | bytes 196640 | tf_op jit(solution)/shard_map/ppermute | solution.py:19
  (133 shorter events, 25.0 us)
Async XLA Ops:
  4.7 9.6 %collective-permute-start = (bf16[64,1536]{1,0:T(8,128)(2,1)}, bf16[64,1536]{1,0:T(8,128)(2,1)S(1)}, u32[]{:S(2)}, u32[]{:S(2)}) collective-permute-start(bf16[64,1536]{1,0:T(8,128)(2,1)} %get-tuple-element.20), channel_id=1, source_target_pairs={{0,12},{4,0},{8,4},{12,8},{1,13},{5,1},{9,5},{13,9},{2,14},{6,2},{... | collective-permute-start | bytes 589832 | tf_op jit(solution)/shard_map/ppermute | solution.py:19
  11.4 16.9 %collective-permute-start.7 = (bf16[192,768]{1,0:T(8,128)(2,1)}, bf16[192,768]{1,0:T(8,128)(2,1)S(1)}, u32[]{:S(2)}, u32[]{:S(2)}) collective-permute-start(bf16[192,768]{1,0:T(8,128)(2,1)} %get-tuple-element.22), channel_id=1, source_target_pairs={{0,1},{1,0},{2,3},{3,2},{4,5},{5,4},{6,7},{7,6},{8,9},{9,8},{10,11... | collective-permute-start | bytes 884744 | tf_op jit(solution)/shard_map/ppermute | solution.py:244
  11.4 16.4 %collective-permute-start.1 = (bf16[64,1536]{1,0:T(8,128)(2,1)}, bf16[64,1536]{1,0:T(8,128)(2,1)S(1)}, u32[]{:S(2)}, u32[]{:S(2)}) collective-permute-start(bf16[64,1536]{1,0:T(8,128)(2,1)} %get-tuple-element.19.refs_0_), channel_id=1, source_target_pairs={{0,1},{1,0},{2,3},{3,2},{4,5},{5,4},{6,7},{7,6},{8,9},{9,8},{10,11... | collective-permute-start | bytes 589832 | tf_op jit(solution)/shard_map/ppermute | solution.py:244
  11.9 16.4 %collective-permute-start.3 = (bf16[64,1536]{1,0:T(8,128)(2,1)}, bf16[64,1536]{1,0:T(8,128)(2,1)S(1)}, u32[]{:S(2)}, u32[]{:S(2)}) collective-permute-start(bf16[64,1536]{1,0:T(8,128)(2,1)} %get-tuple-element.19.refs_0_), channel_id=1, source_target_pairs={{0,2},{1,3},{2,0},{3,1},{4,6},{5,7},{6,4},{7,5},{8,10},{9,11},{10,... | collective-permute-start | bytes 589832 | tf_op jit(solution)/shard_map/ppermute | solution.py:244
  14.3 14.5 %collective-permute-start.4 = (bf16[64,1536]{1,0:T(8,128)(2,1)S(1)}, bf16[64,1536]{1,0:T(8,128)(2,1)S(1)}, u32[]{:S(2)}, u32[]{:S(2)}) collective-permute-start(bf16[64,1536]{1,0:T(8,128)(2,1)S(1)} %collective-permute-done.refs_1_), channel_id=1, source_target_pairs={{0,2},{1,3},{2,0},{3,1},{4,6},{5,7},{6,4},{7,5},{8,10},{9,11},{10,... | collective-permute-start | bytes 589832 | tf_op jit(solution)/shard_map/ppermute | solution.py:244
  16.1 10.2 %collective-permute-start.10 = (bf16[96,768]{1,0:T(8,128)(2,1)}, bf16[96,768]{1,0:T(8,128)(2,1)S(1)}, u32[]{:S(2)}, u32[]{:S(2)}) collective-permute-start(bf16[96,768]{1,0:T(8,128)(2,1)} %get-tuple-element.24), channel_id=1, source_target_pairs={{0,3},{1,2},{2,1},{3,0},{4,7},{5,6},{6,5},{7,4},{8,11},{9,10},{10,... | collective-permute-start | bytes 442376 | tf_op jit(solution)/shard_map/ppermute | solution.py:244
  26.3 6.7 %collective-permute-start.9 = (bf16[96,768]{1,0:T(8,128)(2,1)S(1)}, bf16[96,768]{1,0:T(8,128)(2,1)S(1)}, u32[]{:S(2)}, u32[]{:S(2)}) collective-permute-start(bf16[96,768]{1,0:T(8,128)(2,1)S(1)} %collective-permute-done.8.refs_10_), channel_id=1, source_target_pairs={{0,16},{16,0},{1,17},{17,1},{2,18},{18,2},{3,19},{19,3},{4,20},{20... | collective-permute-start | bytes 442376 | tf_op jit(solution)/shard_map/ppermute | solution.py:244
  27.8 7.9 %collective-permute-start.11 = (bf16[96,768]{1,0:T(8,128)(2,1)S(1)}, bf16[96,768]{1,0:T(8,128)(2,1)S(1)}, u32[]{:S(2)}, u32[]{:S(2)}) collective-permute-start(bf16[96,768]{1,0:T(8,128)(2,1)S(1)} %collective-permute-done.10.refs_12_), channel_id=1, source_target_pairs={{0,16},{16,0},{1,17},{17,1},{2,18},{18,2},{3,19},{19,3},{4,20},{20... | collective-permute-start | bytes 442376 | tf_op jit(solution)/shard_map/ppermute | solution.py:244
  28.3 7.4 %collective-permute-start.2 = (bf16[64,1536]{1,0:T(8,128)(2,1)S(1)}, bf16[64,1536]{1,0:T(8,128)(2,1)S(1)}, u32[]{:S(2)}, u32[]{:S(2)}) collective-permute-start(bf16[64,1536]{1,0:T(8,128)(2,1)S(1)} %collective-permute-done.refs_1_), channel_id=1, source_target_pairs={{0,1},{1,0},{2,3},{3,2},{4,5},{5,4},{6,7},{7,6},{8,9},{9,8},{10,11... | collective-permute-start | bytes 589832 | tf_op jit(solution)/shard_map/ppermute | solution.py:244
  28.4 7.4 %collective-permute-start.5 = (bf16[64,1536]{1,0:T(8,128)(2,1)S(1)}, bf16[64,1536]{1,0:T(8,128)(2,1)S(1)}, u32[]{:S(2)}, u32[]{:S(2)}) collective-permute-start(bf16[64,1536]{1,0:T(8,128)(2,1)S(1)} %collective-permute-done.3.refs_4_), channel_id=1, source_target_pairs={{0,1},{1,0},{2,3},{3,2},{4,5},{5,4},{6,7},{7,6},{8,9},{9,8},{10,11... | collective-permute-start | bytes 589832 | tf_op jit(solution)/shard_map/ppermute | solution.py:244
  28.9 6.9 %collective-permute-start.6 = (bf16[64,1536]{1,0:T(8,128)(2,1)S(1)}, bf16[64,1536]{1,0:T(8,128)(2,1)S(1)}, u32[]{:S(2)}, u32[]{:S(2)}) collective-permute-start(bf16[64,1536]{1,0:T(8,128)(2,1)S(1)} %collective-permute-done.4.refs_5_), channel_id=1, source_target_pairs={{0,1},{1,0},{2,3},{3,2},{4,5},{5,4},{6,7},{7,6},{8,9},{9,8},{10,11... | collective-permute-start | bytes 589832 | tf_op jit(solution)/shard_map/ppermute | solution.py:244
  46.8 8.8 %collective-permute-start.23 = (bf16[4,96,384]{2,1,0:T(8,128)(2,1)}, bf16[4,96,384]{2,1,0:T(8,128)(2,1)S(1)}, u32[]{:S(2)}, u32[]{:S(2)}) collective-permute-start(bf16[4,96,384]{2,1,0:T(8,128)(2,1)} %get-tuple-element.33), channel_id=1, source_target_pairs={{0,16},{16,0},{1,17},{17,1},{2,18},{18,2},{3,19},{19,3},{4,20},{20... | collective-permute-start | bytes 884744 | tf_op jit(solution)/shard_map/ppermute | solution.py:244
  52.9 42.8 %collective-permute-start.12 = (bf16[2,2,64,1536]{3,2,1,0:T(8,128)(2,1)S(1)}, bf16[2,2,64,1536]{3,2,1,0:T(8,128)(2,1)S(1)}, u32[]{:S(2)}, u32[]{:S(2)}) collective-permute-start(bf16[2,2,64,1536]{3,2,1,0:T(8,128)(2,1)S(1)} %get-tuple-element.29), channel_id=1, source_target_pairs={{0,1},{1,0},{2,3},{3,2},{4,5},{5,4},{6,7},{7,6},{8,9},{9,8},{10,11... | collective-permute-start | bytes 2359304 | tf_op jit(solution)/shard_map/ppermute | solution.py:244
  53.0 9.4 %collective-permute-start.15 = (bf16[4,96,384]{2,1,0:T(8,128)(2,1)S(1)}, bf16[4,96,384]{2,1,0:T(8,128)(2,1)S(1)}, u32[]{:S(2)}, u32[]{:S(2)}) collective-permute-start(bf16[4,96,384]{2,1,0:T(8,128)(2,1)S(1)} %copy-done.8), channel_id=1, source_target_pairs={{0,16},{16,0},{1,17},{17,1},{2,18},{18,2},{3,19},{19,3},{4,20},{20... | collective-permute-start | bytes 884744 | tf_op jit(solution)/shard_map/ppermute | solution.py:244
  55.8 6.9 %collective-permute-start.24 = (bf16[4,48,384]{2,1,0:T(8,128)(2,1)S(1)}, bf16[4,48,384]{2,1,0:T(8,128)(2,1)S(1)}, u32[]{:S(2)}, u32[]{:S(2)}) collective-permute-start(bf16[4,48,384]{2,1,0:T(8,128)(2,1)S(1)} %constant_dynamic-slice_fusion.2), channel_id=1, source_target_pairs={{0,4},{4,0},{8,12},{12,8},{1,5},{5,1},{9,13},{13,9},{2,6},{6,2},{1... | collective-permute-start | bytes 442376 | tf_op jit(solution)/shard_map/ppermute | solution.py:244
  62.6 7.0 %collective-permute-start.16 = (bf16[4,48,384]{2,1,0:T(8,128)(2,1)S(1)}, bf16[4,48,384]{2,1,0:T(8,128)(2,1)S(1)}, u32[]{:S(2)}, u32[]{:S(2)}) collective-permute-start(bf16[4,48,384]{2,1,0:T(8,128)(2,1)S(1)} %constant_dynamic-slice_fusion.5), channel_id=1, source_target_pairs={{0,4},{4,0},{8,12},{12,8},{1,5},{5,1},{9,13},{13,9},{2,6},{6,2},{1... | collective-permute-start | bytes 442376 | tf_op jit(solution)/shard_map/ppermute | solution.py:244
  62.7 7.0 %collective-permute-start.25 = (bf16[4,24,384]{2,1,0:T(8,128)(2,1)S(1)}, bf16[4,24,384]{2,1,0:T(8,128)(2,1)S(1)}, u32[]{:S(2)}, u32[]{:S(2)}) collective-permute-start(bf16[4,24,384]{2,1,0:T(8,128)(2,1)S(1)} %constant_dynamic-slice_fusion.1), channel_id=1, source_target_pairs={{0,8},{4,12},{8,0},{12,4},{1,9},{5,13},{9,1},{13,5},{2,10},{6,14},... | collective-permute-start | bytes 221192 | tf_op jit(solution)/shard_map/ppermute | solution.py:244
  79.2 7.6 %collective-permute-start.28 = (bf16[24,1536]{1,0:T(8,128)(2,1)S(1)}, bf16[24,1536]{1,0:T(8,128)(2,1)S(1)}, u32[]{:S(2)}, u32[]{:S(2)}) collective-permute-start(bf16[24,1536]{1,0:T(8,128)(2,1)S(1)} %shard_map.88), channel_id=1, source_target_pairs={{0,8},{4,12},{8,0},{12,4},{1,9},{5,13},{9,1},{13,5},{2,10},{6,14},... | collective-permute-start | bytes 221192 | tf_op jit(solution)/shard_map/ppermute | solution.py:244
  80.4 7.3 %collective-permute-start.20 = (bf16[24,1536]{1,0:T(8,128)(2,1)S(1)}, bf16[24,1536]{1,0:T(8,128)(2,1)S(1)}, u32[]{:S(2)}, u32[]{:S(2)}) collective-permute-start(bf16[24,1536]{1,0:T(8,128)(2,1)S(1)} %shard_map.87), channel_id=1, source_target_pairs={{0,8},{4,12},{8,0},{12,4},{1,9},{5,13},{9,1},{13,5},{2,10},{6,14},... | collective-permute-start | bytes 221192 | tf_op jit(solution)/shard_map/ppermute | solution.py:244
  87.7 6.7 %collective-permute-start.21 = (bf16[48,1536]{1,0:T(8,128)(2,1)S(1)}, bf16[48,1536]{1,0:T(8,128)(2,1)S(1)}, u32[]{:S(2)}, u32[]{:S(2)}) collective-permute-start(bf16[48,1536]{1,0:T(8,128)(2,1)S(1)} %pad_maximum_fusion.4), channel_id=1, source_target_pairs={{0,4},{4,0},{8,12},{12,8},{1,5},{5,1},{9,13},{13,9},{2,6},{6,2},{1... | collective-permute-start | bytes 442376 | tf_op jit(solution)/shard_map/ppermute | solution.py:244
  94.6 9.9 %collective-permute-start.30 = (bf16[96,1536]{1,0:T(8,128)(2,1)S(1)}, bf16[96,1536]{1,0:T(8,128)(2,1)S(1)}, u32[]{:S(2)}, u32[]{:S(2)}) collective-permute-start(bf16[96,1536]{1,0:T(8,128)(2,1)S(1)} %pad_maximum_fusion.3), channel_id=1, source_target_pairs={{0,16},{16,0},{1,17},{17,1},{2,18},{18,2},{3,19},{19,3},{4,20},{20... | collective-permute-start | bytes 884744 | tf_op jit(solution)/shard_map/ppermute | solution.py:244
  96.0 12.8 %collective-permute-start.13 = (bf16[1,2,64,1536]{3,2,1,0:T(8,128)(2,1)S(1)}, bf16[1,2,64,1536]{3,2,1,0:T(8,128)(2,1)S(1)}, u32[]{:S(2)}, u32[]{:S(2)}) collective-permute-start(bf16[1,2,64,1536]{3,2,1,0:T(8,128)(2,1)S(1)} %slice.74), channel_id=1, source_target_pairs={{0,2},{1,3},{2,0},{3,1},{4,6},{5,7},{6,4},{7,5},{8,10},{9,11},{10,... | collective-permute-start | bytes 1179656 | tf_op jit(solution)/shard_map/ppermute | solution.py:244
  97.1 10.5 %collective-permute-start.22 = (bf16[96,1536]{1,0:T(8,128)(2,1)S(1)}, bf16[96,1536]{1,0:T(8,128)(2,1)S(1)}, u32[]{:S(2)}, u32[]{:S(2)}) collective-permute-start(bf16[96,1536]{1,0:T(8,128)(2,1)S(1)} %pad_maximum_fusion.2), channel_id=1, source_target_pairs={{0,16},{16,0},{1,17},{17,1},{2,18},{18,2},{3,19},{19,3},{4,20},{20... | collective-permute-start | bytes 884744 | tf_op jit(solution)/shard_map/ppermute | solution.py:244
  108.9 7.5 %collective-permute-start.14 = (bf16[64,1536]{1,0:T(8,128)(2,1)S(1)}, bf16[64,1536]{1,0:T(8,128)(2,1)S(1)}, u32[]{:S(2)}, u32[]{:S(2)}) collective-permute-start(bf16[64,1536]{1,0:T(8,128)(2,1)S(1)} %get-tuple-element.44), channel_id=1, source_target_pairs={{0,4},{4,8},{8,12},{12,0},{1,5},{5,9},{9,13},{13,1},{2,6},{6,10},{... | collective-permute-start | bytes 589832 | tf_op jit(solution)/shard_map/ppermute | solution.py:19
  (28 other events, 200.7 us)
where the time goes:
time: 118 us
  waiting for transfers between devices  65.2 us (55%)
  starting transfers between devices  25 us (21%)
  Pallas kernels  14.9 us (13%)
  local copies, waits for them, and re-layouts  6.06 us (5%)
  other arithmetic  5.37 us (5%)
    ppermute x29, waiting for transfers between devices, swapped(): lax.ppermute(value, axis, [(source, source ^ mask) for source in range(co...  57.7 us
    ppermute x29, starting transfers between devices, swapped(): lax.ppermute(value, axis, [(source, source ^ mask) for source in range(co...  19.3 us
    pallas_call x5, Pallas kernels, call(): pl.pallas_call(body, out_shape=outs, in_specs=[SMEM_SPEC] * len(scalars)...  14.9 us
    ppermute x2, waiting for transfers between devices, shifted(): return lax.ppermute(value, axis, pairs)  7.52 us
    ppermute x2, starting transfers between devices, shifted(): return lax.ppermute(value, axis, pairs)  5.75 us
    unnamed x43, local copies, waits for them, and re-layouts  4.79 us
  transfers between devices with their start and end apart: 31, of which 19 were waited for; matrix products, arithmetic and copies ran while one was open for 5% of the time, Pallas kernels for 1%

commit v1 on v0

--- a/solution.py
+++ b/solution.py
@@ -290,12 +290,12 @@
     return lax.dot_general(a, b, (((0,), (0,)), ((), ())), preferred_element_type=jnp.float32)
 
 
-def deal_kernel(scal_ref, qkv_any, out_any, in_any, up_any, high_ref, low_ref, *refs):
+def deal_kernel(qkv_any, out_any, in_any, up_any, high_ref, low_ref, *refs):
     *block_refs, qkv_ref, out_ref, sems = refs
     tiles_count = len(block_refs)
     channels = out_ref.shape[1]
     own = channels // tiles_count
-    rep, here = scal_ref[0], scal_ref[1]
+    rep, here = lax.axis_index("rep"), lax.axis_index("tile")
     copies = [
         pltpu.make_async_copy(source.at[level], target.at[:, first : first + channels], sems.at[2 * level + which])
         for level, target in ((0, low_ref), (1, high_ref))
@@ -367,7 +367,7 @@
     return jnp.concatenate(parts, axis=1).astype(jnp.bfloat16)
 
 
-def main_kernel(scal_ref, codes_ref, *refs):
+def main_kernel(codes_ref, *refs):
     *refs, inner_ref, outer_ref, wts, keep_a, send_a, keep_b, send_b, hid, up, rolled, result, fields, sems = refs
     tiles_count = (len(refs) + 2) // 4
     cells_refs = refs[: 2 * tiles_count]
@@ -378,7 +378,8 @@
     rows = channels // tiles_count
     half = rows // 2
     plane = tiles_count * cells
-    wrapped, rep, here = scal_ref[0], scal_ref[1], scal_ref[2]
+    rep, here = lax.axis_index("rep"), lax.axis_index("tile")
+    unwrapped = lax.axis_index("lev") != lax.axis_size("lev") - 1
     copies = []
 
     def fetch(source, target):
@@ -430,7 +431,7 @@
     tokens = 2 * cells
     level_k = lax.broadcasted_iota(jnp.int32, (tokens, tokens), 0) // cells
     level_q = lax.broadcasted_iota(jnp.int32, (tokens, tokens), 1) // cells
-    allowed = jnp.where((level_k == level_q) | (wrapped == 0), 1.0, 0.0)
+    allowed = jnp.where((level_k == level_q) | unwrapped, 1.0, 0.0)
 
     def window(w, carry):
         at = pl.ds(pl.multiple_of(w * cells, cells), cells)
@@ -482,9 +483,9 @@
             ref[k // 2, l, :, channels:] = grad_hidden[at]
 
 
-def column_kernel(here_ref, *refs):
+def column_kernel(*refs):
     *slot_refs, out_ref = refs
-    here = here_ref[0]
+    here = lax.axis_index("tile")
     blocks = in_order([ref[...] for ref in slot_refs], here)
     pieces = []
     for which in range(2):
@@ -563,16 +564,15 @@
         found += [got[0], got[1]]
     rows, cols = part.shape[1:]
     channels = tiles_count * cols // 2
-    here = tile_here.reshape(1).astype(jnp.int32)
-    return call(column_kernel, [low_shape(rows, 2 * channels)], [here], found, 1000, 4)[0]
-
-
-def spread(piece, lev_here, rep_here):
+    return call(column_kernel, [low_shape(rows, 2 * channels)], [], found, 1000, 4)[0]
+
+
+def spread(piece, lev_here):
     for bit in reversed(bits_of(lax.axis_size("lev"))):
         came = swapped(piece, "lev", bit)
         piece = joined(piece, came, (lev_here // bit) % 2)
     came = swapped(piece, "rep", 1)
-    return joined(piece, came, rep_here)
+    return piece, came
 
 
 def shards_by_heads(tokens, w_qkv, w_proj, seam_codes, upstream):
@@ -581,7 +581,6 @@
     tiles_count = lax.axis_size("tile")
     rep_here, lev_here, tile_here = lax.axis_index("rep"), lax.axis_index("lev"), lax.axis_index("tile")
     shard_rows = w_qkv.shape[0]
-    wrapped = lev_here == lax.axis_size("lev") - 1
     field_in = tokens.reshape(levels, cells, channels)
     field_up = upstream.reshape(levels, cells, channels)
     half = shard_rows // 2
@@ -592,7 +591,7 @@
         [shape, shape]
         + [low_shape(shard_rows, channels)] * 2
         + [low_shape(half, channels)] * (tiles_count - 2),
-        [jnp.stack([rep_here.astype(jnp.int32), tile_here.astype(jnp.int32)])],
+        [],
         [w_qkv, w_proj, field_in, field_up],
         1000,
         MAIN_MEBIBYTES,
@@ -618,7 +617,6 @@
         return [have[k] for k in range(tiles_count)]
 
     pieces = [p for pair in zip(gathered(high), gathered(low)) for p in pair]
-    scalars = jnp.stack([wrapped.astype(jnp.int32), rep_here.astype(jnp.int32), tile_here.astype(jnp.int32)])
     plane = tiles_count * cells
     width = 3 * LANES
     part_shape = low_shape(tiles_count, half, width)
@@ -628,7 +626,7 @@
     inner, outer, weight, keep_a, send_a, keep_b, send_b = call(
         main_kernel,
         [inner_shape, outer_shape, weight_shape, part_shape, part_shape, part_shape, part_shape],
-        [scalars, seam_codes],
+        [seam_codes],
         [*pieces, *weights],
         8 * levels * plane * channels * channels,
         MAIN_MEBIBYTES,
@@ -660,12 +658,21 @@
     output = (token_rows.astype(jnp.float32) + final[:, :channels].astype(jnp.float32)).astype(jnp.bfloat16)
     grad_tokens = norm_backward(upstream_rows, final[:, channels:].astype(jnp.float32), normalized, inverse)
 
-    grad_b, grad_a = [
-        spread(reduce_share(*pair, lev_here, tile_here), lev_here, rep_here).astype(jnp.float32)
-        for pair in ((keep_b, send_b), (keep_a, send_a))
+    (own_b, other_b), (own_a, other_a) = [
+        spread(reduce_share(*pair, level, tile), level)
+        for pair, (level, tile) in (
+            ((keep_b, send_b), (lev_here, tile_here)),
+            ((keep_a, send_a), lax.optimization_barrier((lev_here, tile_here))),
+        )
     ]
-    grad_qkv = jnp.concatenate([grad_a, grad_b[:, :channels]], axis=1)
-    grad_proj = grad_b[:, channels:]
+    rows = own_a.shape[0]
+    grad_qkv = jnp.zeros((shard_rows, 3 * channels), jnp.float32)
+    grad_proj = jnp.zeros((shard_rows, channels), jnp.float32)
+    for piece_a, piece_b, at in ((own_a, own_b, rep_here * rows), (other_a, other_b, (1 - rep_here) * rows)):
+        value, out = piece_b[:, :channels].astype(jnp.float32), piece_b[:, channels:].astype(jnp.float32)
+        grad_proj = lax.dynamic_update_slice(grad_proj, out, (at, 0))
+        grad_qkv = lax.dynamic_update_slice(grad_qkv, value, (at, 2 * channels))
+        grad_qkv = lax.dynamic_update_slice(grad_qkv, piece_a.astype(jnp.float32), (at, 0))
     return (output.reshape(tokens.shape), grad_tokens.reshape(tokens.shape), grad_qkv, grad_proj)
 
 

time: 118 us -> 109 us (0.924)
  waiting for transfers between devices: 65.2 us -> 59.1 us
  other arithmetic: 5.37 us -> 3.49 us
    ppermute x29, waiting for transfers between devices: 57.7 us -> 52.6 us  [swapped(): lax.ppermute(value, axis, [(source, source ^ mask) for source in range(co...]
    concatenate x1 -> x0, other arithmetic: 1.32 us -> none  [shards_by_heads(): grad_qkv = jnp.concatenate([grad_a, grad_b[:, :channels]], axis=1)]
    another operation x2 -> x0, other arithmetic: 1.29 us -> none  [the longest x1 0.67 us: shards_by_heads(): jnp.stack([wrapped.astype(jnp.int32), rep_here.astype(jnp.int32), tile_he...]
    unnamed x43 -> x47, local copies, waits for them, and re-layouts: 4.79 us -> 4.83 us
  transfers between devices with their start and end apart: 31 -> 31, of which waited for: 19 -> 19; matrix products, arithmetic and copies ran while one was open for 5% -> 3% of each run, Pallas kernels for 1% -> 1%
where the time goes in v1:
time: 109 us
  waiting for transfers between devices  59.1 us (54%)
  starting transfers between devices  25.4 us (23%)
  Pallas kernels  14.2 us (13%)
  local copies, waits for them, and re-layouts  5.36 us (5%)
  other arithmetic  3.49 us (3%)
  between operations  1.4 us (1%)
    ppermute x29, waiting for transfers between devices, swapped(): lax.ppermute(value, axis, [(source, source ^ mask) for source in range(co...  52.6 us
    ppermute x29, starting transfers between devices, swapped(): lax.ppermute(value, axis, [(source, source ^ mask) for source in range(co...  19.4 us
    pallas_call x5, Pallas kernels, call(): pl.pallas_call(body, out_shape=outs, in_specs=[SMEM_SPEC] * len(scalars)...  14.2 us
    ppermute x2, waiting for transfers between devices, shifted(): return lax.ppermute(value, axis, pairs)  6.46 us
    ppermute x2, starting transfers between devices, shifted(): return lax.ppermute(value, axis, pairs)  5.99 us
    unnamed x47, local copies, waits for them, and re-layouts  4.83 us
  transfers between devices with their start and end apart: 31, of which 19 were waited for; matrix products, arithmetic and copies ran while one was open for 3% of the time, Pallas kernels for 1%

profile of v1, /device:TPU:0, one launch (start us, length us, event | category | flops | bytes accessed | tf_op | source)
XLA Modules:
  0.0 109.0 jit_solution(10965887962938540059)
XLA Ops:
  0.7 2.8 %shard_map.84 = (bf16[64,1536]{1,0:T(8,128)(2,1)}, bf16[64,1536]{1,0:T(8,128)(2,1)}, bf16[192,768]{1,0:T(8,128)(2,1)}, bf16[192,768]{1,0:T(8,128)(2,1)}, bf16[96...) custom-call(bf16[192,2304]{1,0:T(8,128)(2,1)} %qkv_any.1, bf16[192,768]{1,0:T(8,128)(2,1)} %out_any.1, ...), custom_call_target="tpu_custom_call" | custom-call | flops 1000 | bytes 2850816 | tf_op jit(solution)/shard_map/pallas_call | solution.py:506
  3.5 5.1 %collective-permute-start = (bf16[64,1536]{1,0:T(8,128)(2,1)}, bf16[64,1536]{1,0:T(8,128)(2,1)S(1)}, u32[]{:S(2)}, u32[]{:S(2)}) collective-permute-start(bf16[64,1536]{1,0:T(8,128)(2,1)} %get-tuple-element.22), channel_id=1, source_target_pairs={{0,12},{4,0},{8,4},{12,8},{1,13},{5,1},{9,5},{13,9},{2,14},{6,2},{... | collective-permute-start | bytes 589832 | tf_op jit(solution)/shard_map/ppermute | solution.py:19
  8.6 1.5 %collective-permute-start.8 = (bf16[96,768]{1,0:T(8,128)(2,1)}, bf16[96,768]{1,0:T(8,128)(2,1)S(1)}, u32[]{:S(2)}, u32[]{:S(2)}) collective-permute-start(bf16[96,768]{1,0:T(8,128)(2,1)} %get-tuple-element.25), channel_id=1, source_target_pairs={{0,2},{1,3},{2,0},{3,1},{4,6},{5,7},{6,4},{7,5},{8,10},{9,11},{10,... | collective-permute-start | bytes 442376 | tf_op jit(solution)/shard_map/ppermute | solution.py:244
  11.2 1.9 %collective-permute-done.refs_1_ = bf16[64,1536]{1,0:T(8,128)(2,1)S(1)} collective-permute-done((bf16[64,1536]{1,0:T(8,128)(2,1)}, bf16[64,1536]{1,0:T(8,128)(2,1)S(1)}, u32[]{:S(2)}, u32[]{:S(2)}) %collective-permute-start) | collective-permute-done | bytes 196640 | tf_op jit(solution)/shard_map/ppermute | solution.py:19
  13.1 1.5 %collective-permute-start.4 = (bf16[64,1536]{1,0:T(8,128)(2,1)S(1)}, bf16[64,1536]{1,0:T(8,128)(2,1)S(1)}, u32[]{:S(2)}, u32[]{:S(2)}) collective-permute-start(bf16[64,1536]{1,0:T(8,128)(2,1)S(1)} %collective-permute-done.refs_1_), channel_id=1, source_target_pairs={{0,2},{1,3},{2,0},{3,1},{4,6},{5,7},{6,4},{7,5},{8,10},{9,11},{10,... | collective-permute-start | bytes 589832 | tf_op jit(solution)/shard_map/ppermute | solution.py:244
  15.9 9.1 %collective-permute-done.10.refs_12_ = bf16[96,768]{1,0:T(8,128)(2,1)S(1)} collective-permute-done((bf16[96,768]{1,0:T(8,128)(2,1)}, bf16[96,768]{1,0:T(8,128)(2,1)S(1)}, u32[]{:S(2)}, u32[]{:S(2)}) %collective-permute-start.10) | collective-permute-done | bytes 147488 | tf_op jit(solution)/shard_map/ppermute | solution.py:244
  25.0 1.5 %collective-permute-start.9 = (bf16[96,768]{1,0:T(8,128)(2,1)S(1)}, bf16[96,768]{1,0:T(8,128)(2,1)S(1)}, u32[]{:S(2)}, u32[]{:S(2)}) collective-permute-start(bf16[96,768]{1,0:T(8,128)(2,1)S(1)} %collective-permute-done.8.refs_10_), channel_id=1, source_target_pairs={{0,16},{16,0},{1,17},{17,1},{2,18},{18,2},{3,19},{19,3},{4,20},{20... | collective-permute-start | bytes 442376 | tf_op jit(solution)/shard_map/ppermute | solution.py:244
  28.8 3.0 %collective-permute-done.9.refs_11_ = bf16[96,768]{1,0:T(8,128)(2,1)S(1)} collective-permute-done((bf16[96,768]{1,0:T(8,128)(2,1)S(1)}, bf16[96,768]{1,0:T(8,128)(2,1)S(1)}, u32[]{:S(2)}, u32[]{:S(2)}) %collective-permute-start.9) | collective-permute-done | bytes 147488 | tf_op jit(solution)/shard_map/ppermute | solution.py:244
  31.8 2.7 %collective-permute-done.11.refs_13_ = bf16[96,768]{1,0:T(8,128)(2,1)S(1)} collective-permute-done((bf16[96,768]{1,0:T(8,128)(2,1)S(1)}, bf16[96,768]{1,0:T(8,128)(2,1)S(1)}, u32[]{:S(2)}, u32[]{:S(2)}) %collective-permute-start.11) | collective-permute-done | bytes 147488 | tf_op jit(solution)/shard_map/ppermute | solution.py:244
  35.3 10.2 %shard_map.85 = (bf16[512,768]{1,0:T(8,128)(2,1)}, bf16[512,256]{1,0:T(8,128)(2,1)}, bf16[768,768]{1,0:T(8,128)(2,1)}, bf16[4,96,384]{2,1,0:T(8,128)(2,1)}, bf16...) custom-call(s32[4,2]{1,0:T(4,128)} %copy.9.codes_ref, ...), custom_call_target="tpu_custom_call" | custom-call | flops 2415919104 | bytes 6160384 | tf_op jit(solution)/shard_map/pallas_call | solution.py:506
  45.5 1.6 %collective-permute-start.15 = (bf16[4,96,384]{2,1,0:T(8,128)(2,1)}, bf16[4,96,384]{2,1,0:T(8,128)(2,1)S(1)}, u32[]{:S(2)}, u32[]{:S(2)}) collective-permute-start(bf16[4,96,384]{2,1,0:T(8,128)(2,1)} %get-tuple-element.33), channel_id=1, source_target_pairs={{0,16},{16,0},{1,17},{17,1},{2,18},{18,2},{3,19},{19,3},{4,20},{20... | collective-permute-start | bytes 884744 | tf_op jit(solution)/shard_map/ppermute | solution.py:244
  47.3 1.3 %copy-done = bf16[768,768]{1,0:T(8,128)(2,1)S(1)} copy-done((bf16[768,768]{1,0:T(8,128)(2,1)S(1)}, bf16[768,768]{1,0:T(8,128)(2,1)}, u32[]{:S(2)}) %copy-start) | copy-done | bytes 1179672
  52.4 2.0 %collective-permute-done.15 = bf16[4,96,384]{2,1,0:T(8,128)(2,1)S(1)} collective-permute-done((bf16[4,96,384]{2,1,0:T(8,128)(2,1)}, bf16[4,96,384]{2,1,0:T(8,128)(2,1)S(1)}, u32[]{:S(2)}, u32[]{:S(2)}) %collective-permute-start.15) | collective-permute-done | bytes 294944 | tf_op jit(solution)/shard_map/ppermute | solution.py:244
  54.6 6.6 %collective-permute-done.22 = bf16[4,96,384]{2,1,0:T(8,128)(2,1)S(1)} collective-permute-done((bf16[4,96,384]{2,1,0:T(8,128)(2,1)S(1)}, bf16[4,96,384]{2,1,0:T(8,128)(2,1)S(1)}, u32[]{:S(2)}, u32[]{:S(2)}) %collective-permute-start.22) | collective-permute-done | bytes 294944 | tf_op jit(solution)/shard_map/ppermute | solution.py:244
  62.6 5.7 %collective-permute-done.23 = bf16[4,48,384]{2,1,0:T(8,128)(2,1)S(1)} collective-permute-done((bf16[4,48,384]{2,1,0:T(8,128)(2,1)S(1)}, bf16[4,48,384]{2,1,0:T(8,128)(2,1)S(1)}, u32[]{:S(2)}, u32[]{:S(2)}) %collective-permute-start.23) | collective-permute-done | bytes 147488 | tf_op jit(solution)/shard_map/ppermute | solution.py:244
  68.6 5.1 %collective-permute-done.24 = bf16[4,24,384]{2,1,0:T(8,128)(2,1)S(1)} collective-permute-done((bf16[4,24,384]{2,1,0:T(8,128)(2,1)S(1)}, bf16[4,24,384]{2,1,0:T(8,128)(2,1)S(1)}, u32[]{:S(2)}, u32[]{:S(2)}) %collective-permute-start.24) | collective-permute-done | bytes 73760 | tf_op jit(solution)/shard_map/ppermute | solution.py:244
  76.1 1.8 %collective-permute-done.19 = bf16[2,24,384]{2,1,0:T(8,128)(2,1)S(1)} collective-permute-done((bf16[2,24,384]{2,1,0:T(8,128)(2,1)S(1)}, bf16[2,24,384]{2,1,0:T(8,128)(2,1)S(1)}, u32[]{:S(2)}, u32[]{:S(2)}) %collective-permute-start.19) | collective-permute-done | bytes 36896 | tf_op jit(solution)/shard_map/ppermute | solution.py:244
  79.1 2.0 %collective-permute-start.27 = (bf16[24,1536]{1,0:T(8,128)(2,1)S(1)}, bf16[24,1536]{1,0:T(8,128)(2,1)S(1)}, u32[]{:S(2)}, u32[]{:S(2)}) collective-permute-start(bf16[24,1536]{1,0:T(8,128)(2,1)S(1)} %shard_map.88), channel_id=1, source_target_pairs={{0,8},{4,12},{8,0},{12,4},{1,9},{5,13},{9,1},{13,5},{2,10},{6,14},... | collective-permute-start | bytes 221192 | tf_op jit(solution)/shard_map/ppermute | solution.py:244
  81.2 4.4 %collective-permute-done.20 = bf16[24,1536]{1,0:T(8,128)(2,1)S(1)} collective-permute-done((bf16[24,1536]{1,0:T(8,128)(2,1)S(1)}, bf16[24,1536]{1,0:T(8,128)(2,1)S(1)}, u32[]{:S(2)}, u32[]{:S(2)}) %collective-permute-start.20) | collective-permute-done | bytes 73760 | tf_op jit(solution)/shard_map/ppermute | solution.py:244
  86.4 1.3 %collective-permute-start.28 = (bf16[48,1536]{1,0:T(8,128)(2,1)S(1)}, bf16[48,1536]{1,0:T(8,128)(2,1)S(1)}, u32[]{:S(2)}, u32[]{:S(2)}) collective-permute-start(bf16[48,1536]{1,0:T(8,128)(2,1)S(1)} %pad_maximum_fusion.4), channel_id=1, source_target_pairs={{0,4},{4,0},{8,12},{12,8},{1,5},{5,1},{9,13},{13,9},{2,6},{6,2},{1... | collective-permute-start | bytes 442376 | tf_op jit(solution)/shard_map/ppermute | solution.py:244
  89.1 2.5 %collective-permute-done.21 = bf16[48,1536]{1,0:T(8,128)(2,1)S(1)} collective-permute-done((bf16[48,1536]{1,0:T(8,128)(2,1)S(1)}, bf16[48,1536]{1,0:T(8,128)(2,1)S(1)}, u32[]{:S(2)}, u32[]{:S(2)}) %collective-permute-start.21) | collective-permute-done | bytes 147488 | tf_op jit(solution)/shard_map/ppermute | solution.py:244
  94.7 5.3 %collective-permute-done.29 = bf16[96,1536]{1,0:T(8,128)(2,1)S(1)} collective-permute-done((bf16[96,1536]{1,0:T(8,128)(2,1)S(1)}, bf16[96,1536]{1,0:T(8,128)(2,1)S(1)}, u32[]{:S(2)}, u32[]{:S(2)}) %collective-permute-start.29) | collective-permute-done | bytes 294944 | tf_op jit(solution)/shard_map/ppermute | solution.py:244
  101.1 2.1 %collective-permute-done.30 = bf16[96,1536]{1,0:T(8,128)(2,1)S(1)} collective-permute-done((bf16[96,1536]{1,0:T(8,128)(2,1)S(1)}, bf16[96,1536]{1,0:T(8,128)(2,1)S(1)}, u32[]{:S(2)}, u32[]{:S(2)}) %collective-permute-start.30) | collective-permute-done | bytes 294944 | tf_op jit(solution)/shard_map/ppermute | solution.py:244
  103.2 4.5 %collective-permute-done.14 = bf16[64,1536]{1,0:T(8,128)(2,1)S(1)} collective-permute-done((bf16[64,1536]{1,0:T(8,128)(2,1)S(1)}, bf16[64,1536]{1,0:T(8,128)(2,1)S(1)}, u32[]{:S(2)}, u32[]{:S(2)}) %collective-permute-start.14) | collective-permute-done | bytes 196640 | tf_op jit(solution)/shard_map/ppermute | solution.py:19
  (136 shorter events, 21.9 us)
Async XLA Ops:
  3.5 9.6 %collective-permute-start = (bf16[64,1536]{1,0:T(8,128)(2,1)}, bf16[64,1536]{1,0:T(8,128)(2,1)S(1)}, u32[]{:S(2)}, u32[]{:S(2)}) collective-permute-start(bf16[64,1536]{1,0:T(8,128)(2,1)} %get-tuple-element.22), channel_id=1, source_target_pairs={{0,12},{4,0},{8,4},{12,8},{1,13},{5,1},{9,5},{13,9},{2,14},{6,2},{... | collective-permute-start | bytes 589832 | tf_op jit(solution)/shard_map/ppermute | solution.py:19
  10.1 16.9 %collective-permute-start.7 = (bf16[192,768]{1,0:T(8,128)(2,1)}, bf16[192,768]{1,0:T(8,128)(2,1)S(1)}, u32[]{:S(2)}, u32[]{:S(2)}) collective-permute-start(bf16[192,768]{1,0:T(8,128)(2,1)} %get-tuple-element.24), channel_id=1, source_target_pairs={{0,1},{1,0},{2,3},{3,2},{4,5},{5,4},{6,7},{7,6},{8,9},{9,8},{10,11... | collective-permute-start | bytes 884744 | tf_op jit(solution)/shard_map/ppermute | solution.py:244
  10.1 16.4 %collective-permute-start.1 = (bf16[64,1536]{1,0:T(8,128)(2,1)}, bf16[64,1536]{1,0:T(8,128)(2,1)S(1)}, u32[]{:S(2)}, u32[]{:S(2)}) collective-permute-start(bf16[64,1536]{1,0:T(8,128)(2,1)} %get-tuple-element.21.refs_0_), channel_id=1, source_target_pairs={{0,1},{1,0},{2,3},{3,2},{4,5},{5,4},{6,7},{7,6},{8,9},{9,8},{10,11... | collective-permute-start | bytes 589832 | tf_op jit(solution)/shard_map/ppermute | solution.py:244
  10.7 16.4 %collective-permute-start.3 = (bf16[64,1536]{1,0:T(8,128)(2,1)}, bf16[64,1536]{1,0:T(8,128)(2,1)S(1)}, u32[]{:S(2)}, u32[]{:S(2)}) collective-permute-start(bf16[64,1536]{1,0:T(8,128)(2,1)} %get-tuple-element.21.refs_0_), channel_id=1, source_target_pairs={{0,2},{1,3},{2,0},{3,1},{4,6},{5,7},{6,4},{7,5},{8,10},{9,11},{10,... | collective-permute-start | bytes 589832 | tf_op jit(solution)/shard_map/ppermute | solution.py:244
  13.1 14.5 %collective-permute-start.4 = (bf16[64,1536]{1,0:T(8,128)(2,1)S(1)}, bf16[64,1536]{1,0:T(8,128)(2,1)S(1)}, u32[]{:S(2)}, u32[]{:S(2)}) collective-permute-start(bf16[64,1536]{1,0:T(8,128)(2,1)S(1)} %collective-permute-done.refs_1_), channel_id=1, source_target_pairs={{0,2},{1,3},{2,0},{3,1},{4,6},{5,7},{6,4},{7,5},{8,10},{9,11},{10,... | collective-permute-start | bytes 589832 | tf_op jit(solution)/shard_map/ppermute | solution.py:244
  14.8 10.2 %collective-permute-start.10 = (bf16[96,768]{1,0:T(8,128)(2,1)}, bf16[96,768]{1,0:T(8,128)(2,1)S(1)}, u32[]{:S(2)}, u32[]{:S(2)}) collective-permute-start(bf16[96,768]{1,0:T(8,128)(2,1)} %get-tuple-element.26), channel_id=1, source_target_pairs={{0,3},{1,2},{2,1},{3,0},{4,7},{5,6},{6,5},{7,4},{8,11},{9,10},{10,... | collective-permute-start | bytes 442376 | tf_op jit(solution)/shard_map/ppermute | solution.py:244
  25.0 6.7 %collective-permute-start.9 = (bf16[96,768]{1,0:T(8,128)(2,1)S(1)}, bf16[96,768]{1,0:T(8,128)(2,1)S(1)}, u32[]{:S(2)}, u32[]{:S(2)}) collective-permute-start(bf16[96,768]{1,0:T(8,128)(2,1)S(1)} %collective-permute-done.8.refs_10_), channel_id=1, source_target_pairs={{0,16},{16,0},{1,17},{17,1},{2,18},{18,2},{3,19},{19,3},{4,20},{20... | collective-permute-start | bytes 442376 | tf_op jit(solution)/shard_map/ppermute | solution.py:244
  26.5 7.9 %collective-permute-start.11 = (bf16[96,768]{1,0:T(8,128)(2,1)S(1)}, bf16[96,768]{1,0:T(8,128)(2,1)S(1)}, u32[]{:S(2)}, u32[]{:S(2)}) collective-permute-start(bf16[96,768]{1,0:T(8,128)(2,1)S(1)} %collective-permute-done.10.refs_12_), channel_id=1, source_target_pairs={{0,16},{16,0},{1,17},{17,1},{2,18},{18,2},{3,19},{19,3},{4,20},{20... | collective-permute-start | bytes 442376 | tf_op jit(solution)/shard_map/ppermute | solution.py:244
  27.1 7.4 %collective-permute-start.2 = (bf16[64,1536]{1,0:T(8,128)(2,1)S(1)}, bf16[64,1536]{1,0:T(8,128)(2,1)S(1)}, u32[]{:S(2)}, u32[]{:S(2)}) collective-permute-start(bf16[64,1536]{1,0:T(8,128)(2,1)S(1)} %collective-permute-done.refs_1_), channel_id=1, source_target_pairs={{0,1},{1,0},{2,3},{3,2},{4,5},{5,4},{6,7},{7,6},{8,9},{9,8},{10,11... | collective-permute-start | bytes 589832 | tf_op jit(solution)/shard_map/ppermute | solution.py:244
  27.1 7.4 %collective-permute-start.5 = (bf16[64,1536]{1,0:T(8,128)(2,1)S(1)}, bf16[64,1536]{1,0:T(8,128)(2,1)S(1)}, u32[]{:S(2)}, u32[]{:S(2)}) collective-permute-start(bf16[64,1536]{1,0:T(8,128)(2,1)S(1)} %collective-permute-done.3.refs_4_), channel_id=1, source_target_pairs={{0,1},{1,0},{2,3},{3,2},{4,5},{5,4},{6,7},{7,6},{8,9},{9,8},{10,11... | collective-permute-start | bytes 589832 | tf_op jit(solution)/shard_map/ppermute | solution.py:244
  27.6 6.9 %collective-permute-start.6 = (bf16[64,1536]{1,0:T(8,128)(2,1)S(1)}, bf16[64,1536]{1,0:T(8,128)(2,1)S(1)}, u32[]{:S(2)}, u32[]{:S(2)}) collective-permute-start(bf16[64,1536]{1,0:T(8,128)(2,1)S(1)} %collective-permute-done.4.refs_5_), channel_id=1, source_target_pairs={{0,1},{1,0},{2,3},{3,2},{4,5},{5,4},{6,7},{7,6},{8,9},{9,8},{10,11... | collective-permute-start | bytes 589832 | tf_op jit(solution)/shard_map/ppermute | solution.py:244
  45.5 8.8 %collective-permute-start.15 = (bf16[4,96,384]{2,1,0:T(8,128)(2,1)}, bf16[4,96,384]{2,1,0:T(8,128)(2,1)S(1)}, u32[]{:S(2)}, u32[]{:S(2)}) collective-permute-start(bf16[4,96,384]{2,1,0:T(8,128)(2,1)} %get-tuple-element.33), channel_id=1, source_target_pairs={{0,16},{16,0},{1,17},{17,1},{2,18},{18,2},{3,19},{19,3},{4,20},{20... | collective-permute-start | bytes 884744 | tf_op jit(solution)/shard_map/ppermute | solution.py:244
  51.7 36.1 %collective-permute-start.12 = (bf16[2,2,64,1536]{3,2,1,0:T(8,128)(2,1)S(1)}, bf16[2,2,64,1536]{3,2,1,0:T(8,128)(2,1)S(1)}, u32[]{:S(2)}, u32[]{:S(2)}) collective-permute-start(bf16[2,2,64,1536]{3,2,1,0:T(8,128)(2,1)S(1)} %get-tuple-element.31), channel_id=1, source_target_pairs={{0,1},{1,0},{2,3},{3,2},{4,5},{5,4},{6,7},{7,6},{8,9},{9,8},{10,11... | collective-permute-start | bytes 2359304 | tf_op jit(solution)/shard_map/ppermute | solution.py:244
  51.8 9.4 %collective-permute-start.22 = (bf16[4,96,384]{2,1,0:T(8,128)(2,1)S(1)}, bf16[4,96,384]{2,1,0:T(8,128)(2,1)S(1)}, u32[]{:S(2)}, u32[]{:S(2)}) collective-permute-start(bf16[4,96,384]{2,1,0:T(8,128)(2,1)S(1)} %copy-done.11), channel_id=1, source_target_pairs={{0,16},{16,0},{1,17},{17,1},{2,18},{18,2},{3,19},{19,3},{4,20},{20... | collective-permute-start | bytes 884744 | tf_op jit(solution)/shard_map/ppermute | solution.py:244
  54.5 6.9 %collective-permute-start.16 = (bf16[4,48,384]{2,1,0:T(8,128)(2,1)S(1)}, bf16[4,48,384]{2,1,0:T(8,128)(2,1)S(1)}, u32[]{:S(2)}, u32[]{:S(2)}) collective-permute-start(bf16[4,48,384]{2,1,0:T(8,128)(2,1)S(1)} %constant_dynamic-slice_fusion.5), channel_id=1, source_target_pairs={{0,4},{4,0},{8,12},{12,8},{1,5},{5,1},{9,13},{13,9},{2,6},{6,2},{1... | collective-permute-start | bytes 442376 | tf_op jit(solution)/shard_map/ppermute | solution.py:244
  61.3 7.0 %collective-permute-start.23 = (bf16[4,48,384]{2,1,0:T(8,128)(2,1)S(1)}, bf16[4,48,384]{2,1,0:T(8,128)(2,1)S(1)}, u32[]{:S(2)}, u32[]{:S(2)}) collective-permute-start(bf16[4,48,384]{2,1,0:T(8,128)(2,1)S(1)} %constant_dynamic-slice_fusion.2), channel_id=1, source_target_pairs={{0,4},{4,0},{8,12},{12,8},{1,5},{5,1},{9,13},{13,9},{2,6},{6,2},{1... | collective-permute-start | bytes 442376 | tf_op jit(solution)/shard_map/ppermute | solution.py:244
  61.5 7.0 %collective-permute-start.17 = (bf16[4,24,384]{2,1,0:T(8,128)(2,1)S(1)}, bf16[4,24,384]{2,1,0:T(8,128)(2,1)S(1)}, u32[]{:S(2)}, u32[]{:S(2)}) collective-permute-start(bf16[4,24,384]{2,1,0:T(8,128)(2,1)S(1)} %constant_dynamic-slice_fusion.4), channel_id=1, source_target_pairs={{0,8},{4,12},{8,0},{12,4},{1,9},{5,13},{9,1},{13,5},{2,10},{6,14},... | collective-permute-start | bytes 221192 | tf_op jit(solution)/shard_map/ppermute | solution.py:244
  78.0 7.6 %collective-permute-start.20 = (bf16[24,1536]{1,0:T(8,128)(2,1)S(1)}, bf16[24,1536]{1,0:T(8,128)(2,1)S(1)}, u32[]{:S(2)}, u32[]{:S(2)}) collective-permute-start(bf16[24,1536]{1,0:T(8,128)(2,1)S(1)} %shard_map.87), channel_id=1, source_target_pairs={{0,8},{4,12},{8,0},{12,4},{1,9},{5,13},{9,1},{13,5},{2,10},{6,14},... | collective-permute-start | bytes 221192 | tf_op jit(solution)/shard_map/ppermute | solution.py:244
  79.1 7.3 %collective-permute-start.27 = (bf16[24,1536]{1,0:T(8,128)(2,1)S(1)}, bf16[24,1536]{1,0:T(8,128)(2,1)S(1)}, u32[]{:S(2)}, u32[]{:S(2)}) collective-permute-start(bf16[24,1536]{1,0:T(8,128)(2,1)S(1)} %shard_map.88), channel_id=1, source_target_pairs={{0,8},{4,12},{8,0},{12,4},{1,9},{5,13},{9,1},{13,5},{2,10},{6,14},... | collective-permute-start | bytes 221192 | tf_op jit(solution)/shard_map/ppermute | solution.py:244
  86.4 6.7 %collective-permute-start.28 = (bf16[48,1536]{1,0:T(8,128)(2,1)S(1)}, bf16[48,1536]{1,0:T(8,128)(2,1)S(1)}, u32[]{:S(2)}, u32[]{:S(2)}) collective-permute-start(bf16[48,1536]{1,0:T(8,128)(2,1)S(1)} %pad_maximum_fusion.4), channel_id=1, source_target_pairs={{0,4},{4,0},{8,12},{12,8},{1,5},{5,1},{9,13},{13,9},{2,6},{6,2},{1... | collective-permute-start | bytes 442376 | tf_op jit(solution)/shard_map/ppermute | solution.py:244
  88.0 12.1 %collective-permute-start.13 = (bf16[1,2,64,1536]{3,2,1,0:T(8,128)(2,1)S(1)}, bf16[1,2,64,1536]{3,2,1,0:T(8,128)(2,1)S(1)}, u32[]{:S(2)}, u32[]{:S(2)}) collective-permute-start(bf16[1,2,64,1536]{3,2,1,0:T(8,128)(2,1)S(1)} %slice.82), channel_id=1, source_target_pairs={{0,2},{1,3},{2,0},{3,1},{4,6},{5,7},{6,4},{7,5},{8,10},{9,11},{10,... | collective-permute-start | bytes 1179656 | tf_op jit(solution)/shard_map/ppermute | solution.py:244
  91.7 8.3 %collective-permute-start.29 = (bf16[96,1536]{1,0:T(8,128)(2,1)S(1)}, bf16[96,1536]{1,0:T(8,128)(2,1)S(1)}, u32[]{:S(2)}, u32[]{:S(2)}) collective-permute-start(bf16[96,1536]{1,0:T(8,128)(2,1)S(1)} %pad_maximum_fusion.1), channel_id=1, source_target_pairs={{0,16},{16,0},{1,17},{17,1},{2,18},{18,2},{3,19},{19,3},{4,20},{20... | collective-permute-start | bytes 884744 | tf_op jit(solution)/shard_map/ppermute | solution.py:244
  93.3 9.9 %collective-permute-start.30 = (bf16[96,1536]{1,0:T(8,128)(2,1)S(1)}, bf16[96,1536]{1,0:T(8,128)(2,1)S(1)}, u32[]{:S(2)}, u32[]{:S(2)}) collective-permute-start(bf16[96,1536]{1,0:T(8,128)(2,1)S(1)} %pad_maximum_fusion.2), channel_id=1, source_target_pairs={{0,16},{16,0},{1,17},{17,1},{2,18},{18,2},{3,19},{19,3},{4,20},{20... | collective-permute-start | bytes 884744 | tf_op jit(solution)/shard_map/ppermute | solution.py:244
  100.2 7.5 %collective-permute-start.14 = (bf16[64,1536]{1,0:T(8,128)(2,1)S(1)}, bf16[64,1536]{1,0:T(8,128)(2,1)S(1)}, u32[]{:S(2)}, u32[]{:S(2)}) collective-permute-start(bf16[64,1536]{1,0:T(8,128)(2,1)S(1)} %get-tuple-element.42), channel_id=1, source_target_pairs={{0,4},{4,8},{8,12},{12,0},{1,5},{5,9},{9,13},{13,1},{2,6},{6,10},{... | collective-permute-start | bytes 589832 | tf_op jit(solution)/shard_map/ppermute | solution.py:19
  (30 other events, 213.8 us)

commit v2 on v1

--- a/solution.py
+++ b/solution.py
@@ -236,6 +236,7 @@
 
 LANES = 128
 MAIN_MEBIBYTES = 56
+UNROLL = 4
 NEAR = LANES // HEAD_DIM
 
 
@@ -254,7 +255,7 @@
     def code_of(tile, which):
         found = jnp.zeros_like(tile)
         for t in range(tiles_count):
-            found = jnp.where(tile == t, codes_ref[t, which], found)
+            found = jnp.where(tile == t, codes_ref[2 * t + which], found)
         return found == 1
 
     tile = jnp.bitwise_xor(slot, tile_here)
@@ -348,7 +349,7 @@
         k_all, v_all = stacked(k), stacked(v)
         scores = (dot_nt(k_all, q) * scale).reshape(heads, tokens, tokens)
         raised = jnp.exp(scores) * allowed[None]
-        prob = raised / jnp.sum(raised, axis=1, keepdims=True)
+        prob = raised * (1.0 / jnp.sum(raised, axis=1, keepdims=True))
         grad_prob = dot_nt(v_all, o).reshape(heads, tokens, tokens)
         centre = jnp.sum(prob * grad_prob, axis=1, keepdims=True)
         grad_scores = (prob * (grad_prob - centre) * scale).astype(jnp.bfloat16).reshape(-1, tokens)
@@ -441,7 +442,7 @@
         result[1, at, :] = out[cells:]
         return carry
 
-    lax.fori_loop(0, tiles_count, window, 0)
+    lax.fori_loop(0, tiles_count, window, 0, unroll=UNROLL)
 
     zero = jnp.zeros((plane, LANES), jnp.bfloat16)
     for l in range(2):
@@ -467,11 +468,19 @@
             send[j] = jnp.where(rep == 0, second, first)
 
 
-def rows_kernel(inner_ref, outer_ref, wts, keep_ref, send_ref):
+def rows_kernel(inner_any, outer_any, wts_any, keep_ref, send_ref, inner_ref, outer_ref, wts, sems):
     slots, levels, cells, width = keep_ref.shape
     channels = width // 2
     plane = 2 * slots * cells
     split = 4 * LANES
+    copies = [
+        pltpu.make_async_copy(source, target, sems.at[n])
+        for n, (source, target) in enumerate(((inner_any, inner_ref), (outer_any, outer_ref), (wts_any, wts)))
+    ]
+    for copy in copies:
+        copy.start()
+    for copy in copies:
+        copy.wait()
     for l in range(levels):
         at = slice(l * plane, (l + 1) * plane)
         grad_hidden = dot_nt(inner_ref[at, :], wts[...]).astype(jnp.bfloat16)
@@ -602,6 +611,7 @@
         ],
         spec=ANY_SPEC,
     )
+    codes, blocks[1] = lax.optimization_barrier((seam_codes.reshape(-1), blocks[1]))
     low = shifted(low, "lev", -1)
     weights = [blocks[0]]
     for k in range(1, tiles_count):
@@ -626,7 +636,7 @@
     inner, outer, weight, keep_a, send_a, keep_b, send_b = call(
         main_kernel,
         [inner_shape, outer_shape, weight_shape, part_shape, part_shape, part_shape, part_shape],
-        [seam_codes],
+        [codes],
         [*pieces, *weights],
         8 * levels * plane * channels * channels,
         MAIN_MEBIBYTES,
@@ -641,7 +651,21 @@
         spec=ANY_SPEC,
     )
     sums_shape = low_shape(tiles_count // 2, levels, cells, 2 * channels)
-    keep, send = call(rows_kernel, [sums_shape, sums_shape], [], [inner, outer, weight], 10**9, 16)
+    keep, send = call(
+        rows_kernel,
+        [sums_shape, sums_shape],
+        [],
+        [inner, outer, weight],
+        4 * levels * plane * channels * channels // tiles_count,
+        MAIN_MEBIBYTES,
+        scratch=[
+            pltpu.VMEM(inner.shape, jnp.bfloat16),
+            pltpu.VMEM(outer.shape, jnp.bfloat16),
+            pltpu.VMEM(weight.shape, jnp.bfloat16),
+            pltpu.SemaphoreType.DMA((3,)),
+        ],
+        spec=ANY_SPEC,
+    )
 
     came = swapped(send, "tile", 1)
     sums = added(keep, came)

time: 109 us -> 109 us (level)
  local copies, waits for them, and re-layouts: 5.36 us -> 2.8 us
  Pallas kernels: 14.2 us -> 16.3 us
  waiting for transfers between devices: 59.1 us -> 60.2 us
    unnamed x47 -> x41, local copies, waits for them, and re-layouts: 4.83 us -> 1.62 us
    ppermute x29, waiting for transfers between devices: 52.6 us -> 55.1 us  [swapped(): lax.ppermute(value, axis, [(source, source ^ mask) for source in range(co...]
    pallas_call x5, Pallas kernels: 14.2 us -> 16.3 us  [call(): pl.pallas_call(body, out_shape=outs, in_specs=[SMEM_SPEC] * len(scalars)...]
    ppermute x2, waiting for transfers between devices: 6.46 us -> 5.04 us  [shifted(): return lax.ppermute(value, axis, pairs)]
  transfers between devices with their start and end apart: 31 -> 31, of which waited for: 19 -> 18; matrix products, arithmetic and copies ran while one was open for 3% -> 4% of each run, Pallas kernels for 1% -> 4%
where the time goes in v2:
time: 109 us
  waiting for transfers between devices  60.2 us (55%)
  starting transfers between devices  24.7 us (23%)
  Pallas kernels  16.3 us (15%)
  other arithmetic  3.49 us (3%)
  local copies, waits for them, and re-layouts  2.8 us (3%)
  between operations  1.46 us (1%)
    ppermute x29, waiting for transfers between devices, swapped(): lax.ppermute(value, axis, [(source, source ^ mask) for source in range(co...  55.1 us
    ppermute x29, starting transfers between devices, swapped(): lax.ppermute(value, axis, [(source, source ^ mask) for source in range(co...  18.9 us
    pallas_call x5, Pallas kernels, call(): pl.pallas_call(body, out_shape=outs, in_specs=[SMEM_SPEC] * len(scalars)...  16.3 us
    ppermute x2, starting transfers between devices, shifted(): return lax.ppermute(value, axis, pairs)  5.82 us
    ppermute x2, waiting for transfers between devices, shifted(): return lax.ppermute(value, axis, pairs)  5.04 us
  transfers between devices with their start and end apart: 31, of which 18 were waited for; matrix products, arithmetic and copies ran while one was open for 4% of the time, Pallas kernels for 4%

profile of v2, /device:TPU:0, one launch (start us, length us, event | category | flops | bytes accessed | tf_op | source)
XLA Modules:
  0.0 109.0 jit_solution(16643930403584672464)
XLA Ops:
  0.6 2.8 %shard_map.84 = (bf16[64,1536]{1,0:T(8,128)(2,1)}, bf16[64,1536]{1,0:T(8,128)(2,1)}, bf16[192,768]{1,0:T(8,128)(2,1)}, bf16[192,768]{1,0:T(8,128)(2,1)}, bf16[96...) custom-call(bf16[192,2304]{1,0:T(8,128)(2,1)} %qkv_any.1, bf16[192,768]{1,0:T(8,128)(2,1)} %out_any.1, ...), custom_call_target="tpu_custom_call" | custom-call | flops 1000 | bytes 2850816 | tf_op jit(solution)/shard_map/pallas_call | solution.py:515
  3.4 5.1 %collective-permute-start = (bf16[64,1536]{1,0:T(8,128)(2,1)}, bf16[64,1536]{1,0:T(8,128)(2,1)S(1)}, u32[]{:S(2)}, u32[]{:S(2)}) collective-permute-start(bf16[64,1536]{1,0:T(8,128)(2,1)} %get-tuple-element.26), channel_id=1, source_target_pairs={{0,12},{4,0},{8,4},{12,8},{1,13},{5,1},{9,5},{13,9},{2,14},{6,2},{... | collective-permute-start | bytes 589832 | tf_op jit(solution)/shard_map/ppermute | solution.py:19
  8.6 1.5 %collective-permute-start.8 = (bf16[96,768]{1,0:T(8,128)(2,1)}, bf16[96,768]{1,0:T(8,128)(2,1)S(1)}, u32[]{:S(2)}, u32[]{:S(2)}) collective-permute-start(bf16[96,768]{1,0:T(8,128)(2,1)} %get-tuple-element.29), channel_id=1, source_target_pairs={{0,2},{1,3},{2,0},{3,1},{4,6},{5,7},{6,4},{7,5},{8,10},{9,11},{10,... | collective-permute-start | bytes 442376 | tf_op jit(solution)/shard_map/ppermute | solution.py:245
  13.0 1.5 %collective-permute-start.4 = (bf16[64,1536]{1,0:T(8,128)(2,1)S(1)}, bf16[64,1536]{1,0:T(8,128)(2,1)S(1)}, u32[]{:S(2)}, u32[]{:S(2)}) collective-permute-start(bf16[64,1536]{1,0:T(8,128)(2,1)S(1)} %collective-permute-done.refs_1_), channel_id=1, source_target_pairs={{0,2},{1,3},{2,0},{3,1},{4,6},{5,7},{6,4},{7,5},{8,10},{9,11},{10,... | collective-permute-start | bytes 589832 | tf_op jit(solution)/shard_map/ppermute | solution.py:245
  15.7 9.8 %collective-permute-done.10.refs_12_ = bf16[96,768]{1,0:T(8,128)(2,1)S(1)} collective-permute-done((bf16[96,768]{1,0:T(8,128)(2,1)}, bf16[96,768]{1,0:T(8,128)(2,1)S(1)}, u32[]{:S(2)}, u32[]{:S(2)}) %collective-permute-start.10) | collective-permute-done | bytes 147488 | tf_op jit(solution)/shard_map/ppermute | solution.py:245
  25.4 1.5 %collective-permute-start.9 = (bf16[96,768]{1,0:T(8,128)(2,1)S(1)}, bf16[96,768]{1,0:T(8,128)(2,1)S(1)}, u32[]{:S(2)}, u32[]{:S(2)}) collective-permute-start(bf16[96,768]{1,0:T(8,128)(2,1)S(1)} %collective-permute-done.8.refs_10_), channel_id=1, source_target_pairs={{0,16},{16,0},{1,17},{17,1},{2,18},{18,2},{3,19},{19,3},{4,20},{20... | collective-permute-start | bytes 442376 | tf_op jit(solution)/shard_map/ppermute | solution.py:245
  28.2 3.9 %collective-permute-done.9.refs_11_ = bf16[96,768]{1,0:T(8,128)(2,1)S(1)} collective-permute-done((bf16[96,768]{1,0:T(8,128)(2,1)S(1)}, bf16[96,768]{1,0:T(8,128)(2,1)S(1)}, u32[]{:S(2)}, u32[]{:S(2)}) %collective-permute-start.9) | collective-permute-done | bytes 147488 | tf_op jit(solution)/shard_map/ppermute | solution.py:245
  32.2 3.0 %collective-permute-done.11.refs_13_ = bf16[96,768]{1,0:T(8,128)(2,1)S(1)} collective-permute-done((bf16[96,768]{1,0:T(8,128)(2,1)S(1)}, bf16[96,768]{1,0:T(8,128)(2,1)S(1)}, u32[]{:S(2)}, u32[]{:S(2)}) %collective-permute-start.11) | collective-permute-done | bytes 147488 | tf_op jit(solution)/shard_map/ppermute | solution.py:245
  36.1 9.6 %shard_map.85 = (bf16[512,768]{1,0:T(8,128)(2,1)}, bf16[512,256]{1,0:T(8,128)(2,1)}, bf16[768,768]{1,0:T(8,128)(2,1)}, bf16[4,96,384]{2,1,0:T(8,128)(2,1)}, bf16...) custom-call(s32[8]{0:T(128)} %reshape.97.codes_ref, ...), custom_call_target="tpu_custom_call" | custom-call | flops 2415919104 | bytes 6160384 | tf_op jit(solution)/shard_map/pallas_call | solution.py:515
  45.7 1.6 %collective-permute-start.15 = (bf16[4,96,384]{2,1,0:T(8,128)(2,1)}, bf16[4,96,384]{2,1,0:T(8,128)(2,1)S(1)}, u32[]{:S(2)}, u32[]{:S(2)}) collective-permute-start(bf16[4,96,384]{2,1,0:T(8,128)(2,1)} %get-tuple-element.37), channel_id=1, source_target_pairs={{0,16},{16,0},{1,17},{17,1},{2,18},{18,2},{3,19},{19,3},{4,20},{20... | collective-permute-start | bytes 884744 | tf_op jit(solution)/shard_map/ppermute | solution.py:245
  47.9 3.8 %shard_map.86 = (bf16[2,2,64,1536]{3,2,1,0:T(8,128)(2,1)}, bf16[2,2,64,1536]{3,2,1,0:T(8,128)(2,1)}) custom-call(bf16[512,768]{1,0:T(8,128)(2,1)} %get-tuple-element.31.inner_any, bf16[512,256]{1,0:T(8,128)(2,1)} %get-tuple-element.32.outer_any, bf16[768,768]{1,0:T(8,128)(2,1)} %get-tuple-element.33.wts_any), custom_call_target="tpu_custom_call" | custom-call | flops 301989888 | bytes 3801088 | tf_op jit(solution)/shard_map/pallas_call | solution.py:515
  52.3 2.5 %collective-permute-done.15 = bf16[4,96,384]{2,1,0:T(8,128)(2,1)S(1)} collective-permute-done((bf16[4,96,384]{2,1,0:T(8,128)(2,1)}, bf16[4,96,384]{2,1,0:T(8,128)(2,1)S(1)}, u32[]{:S(2)}, u32[]{:S(2)}) %collective-permute-start.15) | collective-permute-done | bytes 294944 | tf_op jit(solution)/shard_map/ppermute | solution.py:245
  55.0 6.1 %collective-permute-done.22 = bf16[4,96,384]{2,1,0:T(8,128)(2,1)S(1)} collective-permute-done((bf16[4,96,384]{2,1,0:T(8,128)(2,1)S(1)}, bf16[4,96,384]{2,1,0:T(8,128)(2,1)S(1)}, u32[]{:S(2)}, u32[]{:S(2)}) %collective-permute-start.22) | collective-permute-done | bytes 294944 | tf_op jit(solution)/shard_map/ppermute | solution.py:245
  62.4 5.9 %collective-permute-done.23 = bf16[4,48,384]{2,1,0:T(8,128)(2,1)S(1)} collective-permute-done((bf16[4,48,384]{2,1,0:T(8,128)(2,1)S(1)}, bf16[4,48,384]{2,1,0:T(8,128)(2,1)S(1)}, u32[]{:S(2)}, u32[]{:S(2)}) %collective-permute-start.23) | collective-permute-done | bytes 147488 | tf_op jit(solution)/shard_map/ppermute | solution.py:245
  68.5 5.1 %collective-permute-done.24 = bf16[4,24,384]{2,1,0:T(8,128)(2,1)S(1)} collective-permute-done((bf16[4,24,384]{2,1,0:T(8,128)(2,1)S(1)}, bf16[4,24,384]{2,1,0:T(8,128)(2,1)S(1)}, u32[]{:S(2)}, u32[]{:S(2)}) %collective-permute-start.24) | collective-permute-done | bytes 73760 | tf_op jit(solution)/shard_map/ppermute | solution.py:245
  76.0 1.9 %collective-permute-done.19 = bf16[2,24,384]{2,1,0:T(8,128)(2,1)S(1)} collective-permute-done((bf16[2,24,384]{2,1,0:T(8,128)(2,1)S(1)}, bf16[2,24,384]{2,1,0:T(8,128)(2,1)S(1)}, u32[]{:S(2)}, u32[]{:S(2)}) %collective-permute-start.19) | collective-permute-done | bytes 36896 | tf_op jit(solution)/shard_map/ppermute | solution.py:245
  79.1 2.0 %collective-permute-start.27 = (bf16[24,1536]{1,0:T(8,128)(2,1)S(1)}, bf16[24,1536]{1,0:T(8,128)(2,1)S(1)}, u32[]{:S(2)}, u32[]{:S(2)}) collective-permute-start(bf16[24,1536]{1,0:T(8,128)(2,1)S(1)} %shard_map.88), channel_id=1, source_target_pairs={{0,8},{4,12},{8,0},{12,4},{1,9},{5,13},{9,1},{13,5},{2,10},{6,14},... | collective-permute-start | bytes 221192 | tf_op jit(solution)/shard_map/ppermute | solution.py:245
  81.1 4.4 %collective-permute-done.20 = bf16[24,1536]{1,0:T(8,128)(2,1)S(1)} collective-permute-done((bf16[24,1536]{1,0:T(8,128)(2,1)S(1)}, bf16[24,1536]{1,0:T(8,128)(2,1)S(1)}, u32[]{:S(2)}, u32[]{:S(2)}) %collective-permute-start.20) | collective-permute-done | bytes 73760 | tf_op jit(solution)/shard_map/ppermute | solution.py:245
  86.4 1.3 %collective-permute-start.28 = (bf16[48,1536]{1,0:T(8,128)(2,1)S(1)}, bf16[48,1536]{1,0:T(8,128)(2,1)S(1)}, u32[]{:S(2)}, u32[]{:S(2)}) collective-permute-start(bf16[48,1536]{1,0:T(8,128)(2,1)S(1)} %pad_maximum_fusion.4), channel_id=1, source_target_pairs={{0,4},{4,0},{8,12},{12,8},{1,5},{5,1},{9,13},{13,9},{2,6},{6,2},{1... | collective-permute-start | bytes 442376 | tf_op jit(solution)/shard_map/ppermute | solution.py:245
  88.8 2.8 %collective-permute-done.21 = bf16[48,1536]{1,0:T(8,128)(2,1)S(1)} collective-permute-done((bf16[48,1536]{1,0:T(8,128)(2,1)S(1)}, bf16[48,1536]{1,0:T(8,128)(2,1)S(1)}, u32[]{:S(2)}, u32[]{:S(2)}) %collective-permute-start.21) | collective-permute-done | bytes 147488 | tf_op jit(solution)/shard_map/ppermute | solution.py:245
  91.7 1.1 %collective-permute-start.29 = (bf16[96,1536]{1,0:T(8,128)(2,1)S(1)}, bf16[96,1536]{1,0:T(8,128)(2,1)S(1)}, u32[]{:S(2)}, u32[]{:S(2)}) collective-permute-start(bf16[96,1536]{1,0:T(8,128)(2,1)S(1)} %pad_maximum_fusion.1), channel_id=1, source_target_pairs={{0,16},{16,0},{1,17},{17,1},{2,18},{18,2},{3,19},{19,3},{4,20},{20... | collective-permute-start | bytes 884744 | tf_op jit(solution)/shard_map/ppermute | solution.py:245
  94.7 5.3 %collective-permute-done.29 = bf16[96,1536]{1,0:T(8,128)(2,1)S(1)} collective-permute-done((bf16[96,1536]{1,0:T(8,128)(2,1)S(1)}, bf16[96,1536]{1,0:T(8,128)(2,1)S(1)}, u32[]{:S(2)}, u32[]{:S(2)}) %collective-permute-start.29) | collective-permute-done | bytes 294944 | tf_op jit(solution)/shard_map/ppermute | solution.py:245
  100.9 2.3 %collective-permute-done.30 = bf16[96,1536]{1,0:T(8,128)(2,1)S(1)} collective-permute-done((bf16[96,1536]{1,0:T(8,128)(2,1)S(1)}, bf16[96,1536]{1,0:T(8,128)(2,1)S(1)}, u32[]{:S(2)}, u32[]{:S(2)}) %collective-permute-start.30) | collective-permute-done | bytes 294944 | tf_op jit(solution)/shard_map/ppermute | solution.py:245
  103.2 4.5 %collective-permute-done.14 = bf16[64,1536]{1,0:T(8,128)(2,1)S(1)} collective-permute-done((bf16[64,1536]{1,0:T(8,128)(2,1)S(1)}, bf16[64,1536]{1,0:T(8,128)(2,1)S(1)}, u32[]{:S(2)}, u32[]{:S(2)}) %collective-permute-start.14) | collective-permute-done | bytes 196640 | tf_op jit(solution)/shard_map/ppermute | solution.py:19
  (131 shorter events, 18.3 us)
Async XLA Ops:
  3.4 9.6 %collective-permute-start = (bf16[64,1536]{1,0:T(8,128)(2,1)}, bf16[64,1536]{1,0:T(8,128)(2,1)S(1)}, u32[]{:S(2)}, u32[]{:S(2)}) collective-permute-start(bf16[64,1536]{1,0:T(8,128)(2,1)} %get-tuple-element.26), channel_id=1, source_target_pairs={{0,12},{4,0},{8,4},{12,8},{1,13},{5,1},{9,5},{13,9},{2,14},{6,2},{... | collective-permute-start | bytes 589832 | tf_op jit(solution)/shard_map/ppermute | solution.py:19
  11.5 16.2 %collective-permute-start.7 = (bf16[192,768]{1,0:T(8,128)(2,1)}, bf16[192,768]{1,0:T(8,128)(2,1)S(1)}, u32[]{:S(2)}, u32[]{:S(2)}) collective-permute-start(bf16[192,768]{1,0:T(8,128)(2,1)} %get-tuple-element.28), channel_id=1, source_target_pairs={{0,1},{1,0},{2,3},{3,2},{4,5},{5,4},{6,7},{7,6},{8,9},{9,8},{10,11... | collective-permute-start | bytes 884744 | tf_op jit(solution)/shard_map/ppermute | solution.py:245
  11.5 15.4 %collective-permute-start.1 = (bf16[64,1536]{1,0:T(8,128)(2,1)}, bf16[64,1536]{1,0:T(8,128)(2,1)S(1)}, u32[]{:S(2)}, u32[]{:S(2)}) collective-permute-start(bf16[64,1536]{1,0:T(8,128)(2,1)} %get-tuple-element.25.refs_0_), channel_id=1, source_target_pairs={{0,1},{1,0},{2,3},{3,2},{4,5},{5,4},{6,7},{7,6},{8,9},{9,8},{10,11... | collective-permute-start | bytes 589832 | tf_op jit(solution)/shard_map/ppermute | solution.py:245
  12.0 15.5 %collective-permute-start.3 = (bf16[64,1536]{1,0:T(8,128)(2,1)}, bf16[64,1536]{1,0:T(8,128)(2,1)S(1)}, u32[]{:S(2)}, u32[]{:S(2)}) collective-permute-start(bf16[64,1536]{1,0:T(8,128)(2,1)} %get-tuple-element.25.refs_0_), channel_id=1, source_target_pairs={{0,2},{1,3},{2,0},{3,1},{4,6},{5,7},{6,4},{7,5},{8,10},{9,11},{10,... | collective-permute-start | bytes 589832 | tf_op jit(solution)/shard_map/ppermute | solution.py:245
  13.0 15.0 %collective-permute-start.4 = (bf16[64,1536]{1,0:T(8,128)(2,1)S(1)}, bf16[64,1536]{1,0:T(8,128)(2,1)S(1)}, u32[]{:S(2)}, u32[]{:S(2)}) collective-permute-start(bf16[64,1536]{1,0:T(8,128)(2,1)S(1)} %collective-permute-done.refs_1_), channel_id=1, source_target_pairs={{0,2},{1,3},{2,0},{3,1},{4,6},{5,7},{6,4},{7,5},{8,10},{9,11},{10,... | collective-permute-start | bytes 589832 | tf_op jit(solution)/shard_map/ppermute | solution.py:245
  14.6 10.9 %collective-permute-start.10 = (bf16[96,768]{1,0:T(8,128)(2,1)}, bf16[96,768]{1,0:T(8,128)(2,1)S(1)}, u32[]{:S(2)}, u32[]{:S(2)}) collective-permute-start(bf16[96,768]{1,0:T(8,128)(2,1)} %get-tuple-element.30), channel_id=1, source_target_pairs={{0,3},{1,2},{2,1},{3,0},{4,7},{5,6},{6,5},{7,4},{8,11},{9,10},{10,... | collective-permute-start | bytes 442376 | tf_op jit(solution)/shard_map/ppermute | solution.py:245
  25.4 6.7 %collective-permute-start.9 = (bf16[96,768]{1,0:T(8,128)(2,1)S(1)}, bf16[96,768]{1,0:T(8,128)(2,1)S(1)}, u32[]{:S(2)}, u32[]{:S(2)}) collective-permute-start(bf16[96,768]{1,0:T(8,128)(2,1)S(1)} %collective-permute-done.8.refs_10_), channel_id=1, source_target_pairs={{0,16},{16,0},{1,17},{17,1},{2,18},{18,2},{3,19},{19,3},{4,20},{20... | collective-permute-start | bytes 442376 | tf_op jit(solution)/shard_map/ppermute | solution.py:245
  26.9 8.2 %collective-permute-start.11 = (bf16[96,768]{1,0:T(8,128)(2,1)S(1)}, bf16[96,768]{1,0:T(8,128)(2,1)S(1)}, u32[]{:S(2)}, u32[]{:S(2)}) collective-permute-start(bf16[96,768]{1,0:T(8,128)(2,1)S(1)} %collective-permute-done.10.refs_12_), channel_id=1, source_target_pairs={{0,16},{16,0},{1,17},{17,1},{2,18},{18,2},{3,19},{19,3},{4,20},{20... | collective-permute-start | bytes 442376 | tf_op jit(solution)/shard_map/ppermute | solution.py:245
  27.5 7.7 %collective-permute-start.2 = (bf16[64,1536]{1,0:T(8,128)(2,1)S(1)}, bf16[64,1536]{1,0:T(8,128)(2,1)S(1)}, u32[]{:S(2)}, u32[]{:S(2)}) collective-permute-start(bf16[64,1536]{1,0:T(8,128)(2,1)S(1)} %collective-permute-done.refs_1_), channel_id=1, source_target_pairs={{0,1},{1,0},{2,3},{3,2},{4,5},{5,4},{6,7},{7,6},{8,9},{9,8},{10,11... | collective-permute-start | bytes 589832 | tf_op jit(solution)/shard_map/ppermute | solution.py:245
  27.7 7.4 %collective-permute-start.5 = (bf16[64,1536]{1,0:T(8,128)(2,1)S(1)}, bf16[64,1536]{1,0:T(8,128)(2,1)S(1)}, u32[]{:S(2)}, u32[]{:S(2)}) collective-permute-start(bf16[64,1536]{1,0:T(8,128)(2,1)S(1)} %collective-permute-done.3.refs_4_), channel_id=1, source_target_pairs={{0,1},{1,0},{2,3},{3,2},{4,5},{5,4},{6,7},{7,6},{8,9},{9,8},{10,11... | collective-permute-start | bytes 589832 | tf_op jit(solution)/shard_map/ppermute | solution.py:245
  28.0 7.2 %collective-permute-start.6 = (bf16[64,1536]{1,0:T(8,128)(2,1)S(1)}, bf16[64,1536]{1,0:T(8,128)(2,1)S(1)}, u32[]{:S(2)}, u32[]{:S(2)}) collective-permute-start(bf16[64,1536]{1,0:T(8,128)(2,1)S(1)} %collective-permute-done.4.refs_5_), channel_id=1, source_target_pairs={{0,1},{1,0},{2,3},{3,2},{4,5},{5,4},{6,7},{7,6},{8,9},{9,8},{10,11... | collective-permute-start | bytes 589832 | tf_op jit(solution)/shard_map/ppermute | solution.py:245
  45.7 9.2 %collective-permute-start.15 = (bf16[4,96,384]{2,1,0:T(8,128)(2,1)}, bf16[4,96,384]{2,1,0:T(8,128)(2,1)S(1)}, u32[]{:S(2)}, u32[]{:S(2)}) collective-permute-start(bf16[4,96,384]{2,1,0:T(8,128)(2,1)} %get-tuple-element.37), channel_id=1, source_target_pairs={{0,16},{16,0},{1,17},{17,1},{2,18},{18,2},{3,19},{19,3},{4,20},{20... | collective-permute-start | bytes 884744 | tf_op jit(solution)/shard_map/ppermute | solution.py:245
  51.7 36.1 %collective-permute-start.12 = (bf16[2,2,64,1536]{3,2,1,0:T(8,128)(2,1)}, bf16[2,2,64,1536]{3,2,1,0:T(8,128)(2,1)S(1)}, u32[]{:S(2)}, u32[]{:S(2)}) collective-permute-start(bf16[2,2,64,1536]{3,2,1,0:T(8,128)(2,1)} %get-tuple-element.35), channel_id=1, source_target_pairs={{0,1},{1,0},{2,3},{3,2},{4,5},{5,4},{6,7},{7,6},{8,9},{9,8},{10,11... | collective-permute-start | bytes 2359304 | tf_op jit(solution)/shard_map/ppermute | solution.py:245
  51.7 9.4 %collective-permute-start.22 = (bf16[4,96,384]{2,1,0:T(8,128)(2,1)S(1)}, bf16[4,96,384]{2,1,0:T(8,128)(2,1)S(1)}, u32[]{:S(2)}, u32[]{:S(2)}) collective-permute-start(bf16[4,96,384]{2,1,0:T(8,128)(2,1)S(1)} %copy-done.7), channel_id=1, source_target_pairs={{0,16},{16,0},{1,17},{17,1},{2,18},{18,2},{3,19},{19,3},{4,20},{20... | collective-permute-start | bytes 884744 | tf_op jit(solution)/shard_map/ppermute | solution.py:245
  55.0 6.4 %collective-permute-start.16 = (bf16[4,48,384]{2,1,0:T(8,128)(2,1)S(1)}, bf16[4,48,384]{2,1,0:T(8,128)(2,1)S(1)}, u32[]{:S(2)}, u32[]{:S(2)}) collective-permute-start(bf16[4,48,384]{2,1,0:T(8,128)(2,1)S(1)} %constant_dynamic-slice_fusion.5), channel_id=1, source_target_pairs={{0,4},{4,0},{8,12},{12,8},{1,5},{5,1},{9,13},{13,9},{2,6},{6,2},{1... | collective-permute-start | bytes 442376 | tf_op jit(solution)/shard_map/ppermute | solution.py:245
  61.3 7.0 %collective-permute-start.23 = (bf16[4,48,384]{2,1,0:T(8,128)(2,1)S(1)}, bf16[4,48,384]{2,1,0:T(8,128)(2,1)S(1)}, u32[]{:S(2)}, u32[]{:S(2)}) collective-permute-start(bf16[4,48,384]{2,1,0:T(8,128)(2,1)S(1)} %constant_dynamic-slice_fusion.2), channel_id=1, source_target_pairs={{0,4},{4,0},{8,12},{12,8},{1,5},{5,1},{9,13},{13,9},{2,6},{6,2},{1... | collective-permute-start | bytes 442376 | tf_op jit(solution)/shard_map/ppermute | solution.py:245
  61.4 6.9 %collective-permute-start.17 = (bf16[4,24,384]{2,1,0:T(8,128)(2,1)S(1)}, bf16[4,24,384]{2,1,0:T(8,128)(2,1)S(1)}, u32[]{:S(2)}, u32[]{:S(2)}) collective-permute-start(bf16[4,24,384]{2,1,0:T(8,128)(2,1)S(1)} %constant_dynamic-slice_fusion.4), channel_id=1, source_target_pairs={{0,8},{4,12},{8,0},{12,4},{1,9},{5,13},{9,1},{13,5},{2,10},{6,14},... | collective-permute-start | bytes 221192 | tf_op jit(solution)/shard_map/ppermute | solution.py:245
  78.0 7.6 %collective-permute-start.20 = (bf16[24,1536]{1,0:T(8,128)(2,1)S(1)}, bf16[24,1536]{1,0:T(8,128)(2,1)S(1)}, u32[]{:S(2)}, u32[]{:S(2)}) collective-permute-start(bf16[24,1536]{1,0:T(8,128)(2,1)S(1)} %shard_map.87), channel_id=1, source_target_pairs={{0,8},{4,12},{8,0},{12,4},{1,9},{5,13},{9,1},{13,5},{2,10},{6,14},... | collective-permute-start | bytes 221192 | tf_op jit(solution)/shard_map/ppermute | solution.py:245
  79.1 7.3 %collective-permute-start.27 = (bf16[24,1536]{1,0:T(8,128)(2,1)S(1)}, bf16[24,1536]{1,0:T(8,128)(2,1)S(1)}, u32[]{:S(2)}, u32[]{:S(2)}) collective-permute-start(bf16[24,1536]{1,0:T(8,128)(2,1)S(1)} %shard_map.88), channel_id=1, source_target_pairs={{0,8},{4,12},{8,0},{12,4},{1,9},{5,13},{9,1},{13,5},{2,10},{6,14},... | collective-permute-start | bytes 221192 | tf_op jit(solution)/shard_map/ppermute | solution.py:245
  86.4 6.7 %collective-permute-start.28 = (bf16[48,1536]{1,0:T(8,128)(2,1)S(1)}, bf16[48,1536]{1,0:T(8,128)(2,1)S(1)}, u32[]{:S(2)}, u32[]{:S(2)}) collective-permute-start(bf16[48,1536]{1,0:T(8,128)(2,1)S(1)} %pad_maximum_fusion.4), channel_id=1, source_target_pairs={{0,4},{4,0},{8,12},{12,8},{1,5},{5,1},{9,13},{13,9},{2,6},{6,2},{1... | collective-permute-start | bytes 442376 | tf_op jit(solution)/shard_map/ppermute | solution.py:245
  88.0 12.1 %collective-permute-start.13 = (bf16[1,2,64,1536]{3,2,1,0:T(8,128)(2,1)S(1)}, bf16[1,2,64,1536]{3,2,1,0:T(8,128)(2,1)S(1)}, u32[]{:S(2)}, u32[]{:S(2)}) collective-permute-start(bf16[1,2,64,1536]{3,2,1,0:T(8,128)(2,1)S(1)} %slice.82), channel_id=1, source_target_pairs={{0,2},{1,3},{2,0},{3,1},{4,6},{5,7},{6,4},{7,5},{8,10},{9,11},{10,... | collective-permute-start | bytes 1179656 | tf_op jit(solution)/shard_map/ppermute | solution.py:245
  91.7 8.3 %collective-permute-start.29 = (bf16[96,1536]{1,0:T(8,128)(2,1)S(1)}, bf16[96,1536]{1,0:T(8,128)(2,1)S(1)}, u32[]{:S(2)}, u32[]{:S(2)}) collective-permute-start(bf16[96,1536]{1,0:T(8,128)(2,1)S(1)} %pad_maximum_fusion.1), channel_id=1, source_target_pairs={{0,16},{16,0},{1,17},{17,1},{2,18},{18,2},{3,19},{19,3},{4,20},{20... | collective-permute-start | bytes 884744 | tf_op jit(solution)/shard_map/ppermute | solution.py:245
  93.2 9.9 %collective-permute-start.30 = (bf16[96,1536]{1,0:T(8,128)(2,1)S(1)}, bf16[96,1536]{1,0:T(8,128)(2,1)S(1)}, u32[]{:S(2)}, u32[]{:S(2)}) collective-permute-start(bf16[96,1536]{1,0:T(8,128)(2,1)S(1)} %pad_maximum_fusion.2), channel_id=1, source_target_pairs={{0,16},{16,0},{1,17},{17,1},{2,18},{18,2},{3,19},{19,3},{4,20},{20... | collective-permute-start | bytes 884744 | tf_op jit(solution)/shard_map/ppermute | solution.py:245
  100.2 7.5 %collective-permute-start.14 = (bf16[64,1536]{1,0:T(8,128)(2,1)S(1)}, bf16[64,1536]{1,0:T(8,128)(2,1)S(1)}, u32[]{:S(2)}, u32[]{:S(2)}) collective-permute-start(bf16[64,1536]{1,0:T(8,128)(2,1)S(1)} %get-tuple-element.46), channel_id=1, source_target_pairs={{0,4},{4,8},{8,12},{12,0},{1,5},{5,9},{9,13},{13,1},{2,6},{6,10},{... | collective-permute-start | bytes 589832 | tf_op jit(solution)/shard_map/ppermute | solution.py:19
  (27 other events, 209.3 us)

commit v3 on v2

--- a/solution.py
+++ b/solution.py
@@ -302,11 +302,13 @@
         for level, target in ((0, low_ref), (1, high_ref))
         for which, (source, first) in enumerate(((in_any, 0), (up_any, channels)))
     ]
-    copies.append(pltpu.make_async_copy(qkv_any, qkv_ref, sems.at[4]))
-    copies.append(pltpu.make_async_copy(out_any, out_ref, sems.at[5]))
-    for copy in copies:
+    whole = [
+        pltpu.make_async_copy(qkv_any, qkv_ref, sems.at[4]),
+        pltpu.make_async_copy(out_any, out_ref, sems.at[5]),
+    ]
+    for copy in [*whole, *copies]:
         copy.start()
-    for copy in copies:
+    for copy in whole:
         copy.wait()
 
     def columns(which, tile):
@@ -323,6 +325,8 @@
             half = block.shape[0] // 2
             block = jnp.where(rep == 0, block[:half], block[half:])
         ref[...] = block
+    for copy in copies:
+        copy.wait()
 
 
 def attend_window(block, allowed):

time: 109 us -> 109 us (level)
  no operation moved by 1% of the time
where the time goes in v3:
time: 109 us
  waiting for transfers between devices  60.2 us (55%)
  starting transfers between devices  24.7 us (23%)
  Pallas kernels  16.3 us (15%)
  other arithmetic  3.49 us (3%)
  local copies, waits for them, and re-layouts  2.8 us (3%)
  between operations  1.46 us (1%)
    ppermute x29, waiting for transfers between devices, swapped(): lax.ppermute(value, axis, [(source, source ^ mask) for source in range(co...  55.2 us
    ppermute x29, starting transfers between devices, swapped(): lax.ppermute(value, axis, [(source, source ^ mask) for source in range(co...  18.8 us
    pallas_call x5, Pallas kernels, call(): pl.pallas_call(body, out_shape=outs, in_specs=[SMEM_SPEC] * len(scalars)...  16.3 us
    ppermute x2, starting transfers between devices, shifted(): return lax.ppermute(value, axis, pairs)  5.8 us
    ppermute x2, waiting for transfers between devices, shifted(): return lax.ppermute(value, axis, pairs)  5.04 us
  transfers between devices with their start and end apart: 31, of which 18 were waited for; matrix products, arithmetic and copies ran while one was open for 4% of the time, Pallas kernels for 4%

profile of v3, /device:TPU:0, one launch (start us, length us, event | category | flops | bytes accessed | tf_op | source)
XLA Modules:
  0.0 108.9 jit_solution(5380302930279654841)
XLA Ops:
  0.6 2.7 %shard_map.84 = (bf16[64,1536]{1,0:T(8,128)(2,1)}, bf16[64,1536]{1,0:T(8,128)(2,1)}, bf16[192,768]{1,0:T(8,128)(2,1)}, bf16[192,768]{1,0:T(8,128)(2,1)}, bf16[96...) custom-call(bf16[192,2304]{1,0:T(8,128)(2,1)} %qkv_any.1, bf16[192,768]{1,0:T(8,128)(2,1)} %out_any.1, ...), custom_call_target="tpu_custom_call" | custom-call | flops 1000 | bytes 2850816 | tf_op jit(solution)/shard_map/pallas_call | solution.py:519
  3.4 5.1 %collective-permute-start = (bf16[64,1536]{1,0:T(8,128)(2,1)}, bf16[64,1536]{1,0:T(8,128)(2,1)S(1)}, u32[]{:S(2)}, u32[]{:S(2)}) collective-permute-start(bf16[64,1536]{1,0:T(8,128)(2,1)} %get-tuple-element.26), channel_id=1, source_target_pairs={{0,12},{4,0},{8,4},{12,8},{1,13},{5,1},{9,5},{13,9},{2,14},{6,2},{... | collective-permute-start | bytes 589832 | tf_op jit(solution)/shard_map/ppermute | solution.py:19
  8.5 1.5 %collective-permute-start.8 = (bf16[96,768]{1,0:T(8,128)(2,1)}, bf16[96,768]{1,0:T(8,128)(2,1)S(1)}, u32[]{:S(2)}, u32[]{:S(2)}) collective-permute-start(bf16[96,768]{1,0:T(8,128)(2,1)} %get-tuple-element.29), channel_id=1, source_target_pairs={{0,2},{1,3},{2,0},{3,1},{4,6},{5,7},{6,4},{7,5},{8,10},{9,11},{10,... | collective-permute-start | bytes 442376 | tf_op jit(solution)/shard_map/ppermute | solution.py:245
  13.0 1.5 %collective-permute-start.4 = (bf16[64,1536]{1,0:T(8,128)(2,1)S(1)}, bf16[64,1536]{1,0:T(8,128)(2,1)S(1)}, u32[]{:S(2)}, u32[]{:S(2)}) collective-permute-start(bf16[64,1536]{1,0:T(8,128)(2,1)S(1)} %collective-permute-done.refs_1_), channel_id=1, source_target_pairs={{0,2},{1,3},{2,0},{3,1},{4,6},{5,7},{6,4},{7,5},{8,10},{9,11},{10,... | collective-permute-start | bytes 589832 | tf_op jit(solution)/shard_map/ppermute | solution.py:245
  15.6 9.8 %collective-permute-done.10.refs_12_ = bf16[96,768]{1,0:T(8,128)(2,1)S(1)} collective-permute-done((bf16[96,768]{1,0:T(8,128)(2,1)}, bf16[96,768]{1,0:T(8,128)(2,1)S(1)}, u32[]{:S(2)}, u32[]{:S(2)}) %collective-permute-start.10) | collective-permute-done | bytes 147488 | tf_op jit(solution)/shard_map/ppermute | solution.py:245
  25.4 1.5 %collective-permute-start.9 = (bf16[96,768]{1,0:T(8,128)(2,1)S(1)}, bf16[96,768]{1,0:T(8,128)(2,1)S(1)}, u32[]{:S(2)}, u32[]{:S(2)}) collective-permute-start(bf16[96,768]{1,0:T(8,128)(2,1)S(1)} %collective-permute-done.8.refs_10_), channel_id=1, source_target_pairs={{0,16},{16,0},{1,17},{17,1},{2,18},{18,2},{3,19},{19,3},{4,20},{20... | collective-permute-start | bytes 442376 | tf_op jit(solution)/shard_map/ppermute | solution.py:245
  28.2 3.9 %collective-permute-done.9.refs_11_ = bf16[96,768]{1,0:T(8,128)(2,1)S(1)} collective-permute-done((bf16[96,768]{1,0:T(8,128)(2,1)S(1)}, bf16[96,768]{1,0:T(8,128)(2,1)S(1)}, u32[]{:S(2)}, u32[]{:S(2)}) %collective-permute-start.9) | collective-permute-done | bytes 147488 | tf_op jit(solution)/shard_map/ppermute | solution.py:245
  32.1 3.0 %collective-permute-done.11.refs_13_ = bf16[96,768]{1,0:T(8,128)(2,1)S(1)} collective-permute-done((bf16[96,768]{1,0:T(8,128)(2,1)S(1)}, bf16[96,768]{1,0:T(8,128)(2,1)S(1)}, u32[]{:S(2)}, u32[]{:S(2)}) %collective-permute-start.11) | collective-permute-done | bytes 147488 | tf_op jit(solution)/shard_map/ppermute | solution.py:245
  36.0 9.6 %shard_map.85 = (bf16[512,768]{1,0:T(8,128)(2,1)}, bf16[512,256]{1,0:T(8,128)(2,1)}, bf16[768,768]{1,0:T(8,128)(2,1)}, bf16[4,96,384]{2,1,0:T(8,128)(2,1)}, bf16...) custom-call(s32[8]{0:T(128)} %reshape.97.codes_ref, ...), custom_call_target="tpu_custom_call" | custom-call | flops 2415919104 | bytes 6160384 | tf_op jit(solution)/shard_map/pallas_call | solution.py:519
  45.6 1.6 %collective-permute-start.15 = (bf16[4,96,384]{2,1,0:T(8,128)(2,1)}, bf16[4,96,384]{2,1,0:T(8,128)(2,1)S(1)}, u32[]{:S(2)}, u32[]{:S(2)}) collective-permute-start(bf16[4,96,384]{2,1,0:T(8,128)(2,1)} %get-tuple-element.37), channel_id=1, source_target_pairs={{0,16},{16,0},{1,17},{17,1},{2,18},{18,2},{3,19},{19,3},{4,20},{20... | collective-permute-start | bytes 884744 | tf_op jit(solution)/shard_map/ppermute | solution.py:245
  47.8 3.8 %shard_map.86 = (bf16[2,2,64,1536]{3,2,1,0:T(8,128)(2,1)}, bf16[2,2,64,1536]{3,2,1,0:T(8,128)(2,1)}) custom-call(bf16[512,768]{1,0:T(8,128)(2,1)} %get-tuple-element.31.inner_any, bf16[512,256]{1,0:T(8,128)(2,1)} %get-tuple-element.32.outer_any, bf16[768,768]{1,0:T(8,128)(2,1)} %get-tuple-element.33.wts_any), custom_call_target="tpu_custom_call" | custom-call | flops 301989888 | bytes 3801088 | tf_op jit(solution)/shard_map/pallas_call | solution.py:519
  52.3 2.5 %collective-permute-done.15 = bf16[4,96,384]{2,1,0:T(8,128)(2,1)S(1)} collective-permute-done((bf16[4,96,384]{2,1,0:T(8,128)(2,1)}, bf16[4,96,384]{2,1,0:T(8,128)(2,1)S(1)}, u32[]{:S(2)}, u32[]{:S(2)}) %collective-permute-start.15) | collective-permute-done | bytes 294944 | tf_op jit(solution)/shard_map/ppermute | solution.py:245
  55.0 6.1 %collective-permute-done.22 = bf16[4,96,384]{2,1,0:T(8,128)(2,1)S(1)} collective-permute-done((bf16[4,96,384]{2,1,0:T(8,128)(2,1)S(1)}, bf16[4,96,384]{2,1,0:T(8,128)(2,1)S(1)}, u32[]{:S(2)}, u32[]{:S(2)}) %collective-permute-start.22) | collective-permute-done | bytes 294944 | tf_op jit(solution)/shard_map/ppermute | solution.py:245
  62.3 5.9 %collective-permute-done.23 = bf16[4,48,384]{2,1,0:T(8,128)(2,1)S(1)} collective-permute-done((bf16[4,48,384]{2,1,0:T(8,128)(2,1)S(1)}, bf16[4,48,384]{2,1,0:T(8,128)(2,1)S(1)}, u32[]{:S(2)}, u32[]{:S(2)}) %collective-permute-start.23) | collective-permute-done | bytes 147488 | tf_op jit(solution)/shard_map/ppermute | solution.py:245
  68.5 5.1 %collective-permute-done.24 = bf16[4,24,384]{2,1,0:T(8,128)(2,1)S(1)} collective-permute-done((bf16[4,24,384]{2,1,0:T(8,128)(2,1)S(1)}, bf16[4,24,384]{2,1,0:T(8,128)(2,1)S(1)}, u32[]{:S(2)}, u32[]{:S(2)}) %collective-permute-start.24) | collective-permute-done | bytes 73760 | tf_op jit(solution)/shard_map/ppermute | solution.py:245
  75.9 1.9 %collective-permute-done.19 = bf16[2,24,384]{2,1,0:T(8,128)(2,1)S(1)} collective-permute-done((bf16[2,24,384]{2,1,0:T(8,128)(2,1)S(1)}, bf16[2,24,384]{2,1,0:T(8,128)(2,1)S(1)}, u32[]{:S(2)}, u32[]{:S(2)}) %collective-permute-start.19) | collective-permute-done | bytes 36896 | tf_op jit(solution)/shard_map/ppermute | solution.py:245
  79.1 2.0 %collective-permute-start.27 = (bf16[24,1536]{1,0:T(8,128)(2,1)S(1)}, bf16[24,1536]{1,0:T(8,128)(2,1)S(1)}, u32[]{:S(2)}, u32[]{:S(2)}) collective-permute-start(bf16[24,1536]{1,0:T(8,128)(2,1)S(1)} %shard_map.88), channel_id=1, source_target_pairs={{0,8},{4,12},{8,0},{12,4},{1,9},{5,13},{9,1},{13,5},{2,10},{6,14},... | collective-permute-start | bytes 221192 | tf_op jit(solution)/shard_map/ppermute | solution.py:245
  81.1 4.4 %collective-permute-done.20 = bf16[24,1536]{1,0:T(8,128)(2,1)S(1)} collective-permute-done((bf16[24,1536]{1,0:T(8,128)(2,1)S(1)}, bf16[24,1536]{1,0:T(8,128)(2,1)S(1)}, u32[]{:S(2)}, u32[]{:S(2)}) %collective-permute-start.20) | collective-permute-done | bytes 73760 | tf_op jit(solution)/shard_map/ppermute | solution.py:245
  86.4 1.3 %collective-permute-start.28 = (bf16[48,1536]{1,0:T(8,128)(2,1)S(1)}, bf16[48,1536]{1,0:T(8,128)(2,1)S(1)}, u32[]{:S(2)}, u32[]{:S(2)}) collective-permute-start(bf16[48,1536]{1,0:T(8,128)(2,1)S(1)} %pad_maximum_fusion.4), channel_id=1, source_target_pairs={{0,4},{4,0},{8,12},{12,8},{1,5},{5,1},{9,13},{13,9},{2,6},{6,2},{1... | collective-permute-start | bytes 442376 | tf_op jit(solution)/shard_map/ppermute | solution.py:245
  88.8 2.8 %collective-permute-done.21 = bf16[48,1536]{1,0:T(8,128)(2,1)S(1)} collective-permute-done((bf16[48,1536]{1,0:T(8,128)(2,1)S(1)}, bf16[48,1536]{1,0:T(8,128)(2,1)S(1)}, u32[]{:S(2)}, u32[]{:S(2)}) %collective-permute-start.21) | collective-permute-done | bytes 147488 | tf_op jit(solution)/shard_map/ppermute | solution.py:245
  91.6 1.1 %collective-permute-start.29 = (bf16[96,1536]{1,0:T(8,128)(2,1)S(1)}, bf16[96,1536]{1,0:T(8,128)(2,1)S(1)}, u32[]{:S(2)}, u32[]{:S(2)}) collective-permute-start(bf16[96,1536]{1,0:T(8,128)(2,1)S(1)} %pad_maximum_fusion.1), channel_id=1, source_target_pairs={{0,16},{16,0},{1,17},{17,1},{2,18},{18,2},{3,19},{19,3},{4,20},{20... | collective-permute-start | bytes 884744 | tf_op jit(solution)/shard_map/ppermute | solution.py:245
  94.6 5.3 %collective-permute-done.29 = bf16[96,1536]{1,0:T(8,128)(2,1)S(1)} collective-permute-done((bf16[96,1536]{1,0:T(8,128)(2,1)S(1)}, bf16[96,1536]{1,0:T(8,128)(2,1)S(1)}, u32[]{:S(2)}, u32[]{:S(2)}) %collective-permute-start.29) | collective-permute-done | bytes 294944 | tf_op jit(solution)/shard_map/ppermute | solution.py:245
  100.8 2.3 %collective-permute-done.30 = bf16[96,1536]{1,0:T(8,128)(2,1)S(1)} collective-permute-done((bf16[96,1536]{1,0:T(8,128)(2,1)S(1)}, bf16[96,1536]{1,0:T(8,128)(2,1)S(1)}, u32[]{:S(2)}, u32[]{:S(2)}) %collective-permute-start.30) | collective-permute-done | bytes 294944 | tf_op jit(solution)/shard_map/ppermute | solution.py:245
  103.2 4.5 %collective-permute-done.14 = bf16[64,1536]{1,0:T(8,128)(2,1)S(1)} collective-permute-done((bf16[64,1536]{1,0:T(8,128)(2,1)S(1)}, bf16[64,1536]{1,0:T(8,128)(2,1)S(1)}, u32[]{:S(2)}, u32[]{:S(2)}) %collective-permute-start.14) | collective-permute-done | bytes 196640 | tf_op jit(solution)/shard_map/ppermute | solution.py:19
  (131 shorter events, 18.2 us)
Async XLA Ops:
  3.4 9.6 %collective-permute-start = (bf16[64,1536]{1,0:T(8,128)(2,1)}, bf16[64,1536]{1,0:T(8,128)(2,1)S(1)}, u32[]{:S(2)}, u32[]{:S(2)}) collective-permute-start(bf16[64,1536]{1,0:T(8,128)(2,1)} %get-tuple-element.26), channel_id=1, source_target_pairs={{0,12},{4,0},{8,4},{12,8},{1,13},{5,1},{9,5},{13,9},{2,14},{6,2},{... | collective-permute-start | bytes 589832 | tf_op jit(solution)/shard_map/ppermute | solution.py:19
  11.4 16.2 %collective-permute-start.7 = (bf16[192,768]{1,0:T(8,128)(2,1)}, bf16[192,768]{1,0:T(8,128)(2,1)S(1)}, u32[]{:S(2)}, u32[]{:S(2)}) collective-permute-start(bf16[192,768]{1,0:T(8,128)(2,1)} %get-tuple-element.28), channel_id=1, source_target_pairs={{0,1},{1,0},{2,3},{3,2},{4,5},{5,4},{6,7},{7,6},{8,9},{9,8},{10,11... | collective-permute-start | bytes 884744 | tf_op jit(solution)/shard_map/ppermute | solution.py:245
  11.4 15.4 %collective-permute-start.1 = (bf16[64,1536]{1,0:T(8,128)(2,1)}, bf16[64,1536]{1,0:T(8,128)(2,1)S(1)}, u32[]{:S(2)}, u32[]{:S(2)}) collective-permute-start(bf16[64,1536]{1,0:T(8,128)(2,1)} %get-tuple-element.25.refs_0_), channel_id=1, source_target_pairs={{0,1},{1,0},{2,3},{3,2},{4,5},{5,4},{6,7},{7,6},{8,9},{9,8},{10,11... | collective-permute-start | bytes 589832 | tf_op jit(solution)/shard_map/ppermute | solution.py:245
  12.0 15.5 %collective-permute-start.3 = (bf16[64,1536]{1,0:T(8,128)(2,1)}, bf16[64,1536]{1,0:T(8,128)(2,1)S(1)}, u32[]{:S(2)}, u32[]{:S(2)}) collective-permute-start(bf16[64,1536]{1,0:T(8,128)(2,1)} %get-tuple-element.25.refs_0_), channel_id=1, source_target_pairs={{0,2},{1,3},{2,0},{3,1},{4,6},{5,7},{6,4},{7,5},{8,10},{9,11},{10,... | collective-permute-start | bytes 589832 | tf_op jit(solution)/shard_map/ppermute | solution.py:245
  13.0 15.0 %collective-permute-start.4 = (bf16[64,1536]{1,0:T(8,128)(2,1)S(1)}, bf16[64,1536]{1,0:T(8,128)(2,1)S(1)}, u32[]{:S(2)}, u32[]{:S(2)}) collective-permute-start(bf16[64,1536]{1,0:T(8,128)(2,1)S(1)} %collective-permute-done.refs_1_), channel_id=1, source_target_pairs={{0,2},{1,3},{2,0},{3,1},{4,6},{5,7},{6,4},{7,5},{8,10},{9,11},{10,... | collective-permute-start | bytes 589832 | tf_op jit(solution)/shard_map/ppermute | solution.py:245
  14.5 10.9 %collective-permute-start.10 = (bf16[96,768]{1,0:T(8,128)(2,1)}, bf16[96,768]{1,0:T(8,128)(2,1)S(1)}, u32[]{:S(2)}, u32[]{:S(2)}) collective-permute-start(bf16[96,768]{1,0:T(8,128)(2,1)} %get-tuple-element.30), channel_id=1, source_target_pairs={{0,3},{1,2},{2,1},{3,0},{4,7},{5,6},{6,5},{7,4},{8,11},{9,10},{10,... | collective-permute-start | bytes 442376 | tf_op jit(solution)/shard_map/ppermute | solution.py:245
  25.4 6.7 %collective-permute-start.9 = (bf16[96,768]{1,0:T(8,128)(2,1)S(1)}, bf16[96,768]{1,0:T(8,128)(2,1)S(1)}, u32[]{:S(2)}, u32[]{:S(2)}) collective-permute-start(bf16[96,768]{1,0:T(8,128)(2,1)S(1)} %collective-permute-done.8.refs_10_), channel_id=1, source_target_pairs={{0,16},{16,0},{1,17},{17,1},{2,18},{18,2},{3,19},{19,3},{4,20},{20... | collective-permute-start | bytes 442376 | tf_op jit(solution)/shard_map/ppermute | solution.py:245
  26.9 8.2 %collective-permute-start.11 = (bf16[96,768]{1,0:T(8,128)(2,1)S(1)}, bf16[96,768]{1,0:T(8,128)(2,1)S(1)}, u32[]{:S(2)}, u32[]{:S(2)}) collective-permute-start(bf16[96,768]{1,0:T(8,128)(2,1)S(1)} %collective-permute-done.10.refs_12_), channel_id=1, source_target_pairs={{0,16},{16,0},{1,17},{17,1},{2,18},{18,2},{3,19},{19,3},{4,20},{20... | collective-permute-start | bytes 442376 | tf_op jit(solution)/shard_map/ppermute | solution.py:245
  27.4 7.7 %collective-permute-start.2 = (bf16[64,1536]{1,0:T(8,128)(2,1)S(1)}, bf16[64,1536]{1,0:T(8,128)(2,1)S(1)}, u32[]{:S(2)}, u32[]{:S(2)}) collective-permute-start(bf16[64,1536]{1,0:T(8,128)(2,1)S(1)} %collective-permute-done.refs_1_), channel_id=1, source_target_pairs={{0,1},{1,0},{2,3},{3,2},{4,5},{5,4},{6,7},{7,6},{8,9},{9,8},{10,11... | collective-permute-start | bytes 589832 | tf_op jit(solution)/shard_map/ppermute | solution.py:245
  27.7 7.4 %collective-permute-start.5 = (bf16[64,1536]{1,0:T(8,128)(2,1)S(1)}, bf16[64,1536]{1,0:T(8,128)(2,1)S(1)}, u32[]{:S(2)}, u32[]{:S(2)}) collective-permute-start(bf16[64,1536]{1,0:T(8,128)(2,1)S(1)} %collective-permute-done.3.refs_4_), channel_id=1, source_target_pairs={{0,1},{1,0},{2,3},{3,2},{4,5},{5,4},{6,7},{7,6},{8,9},{9,8},{10,11... | collective-permute-start | bytes 589832 | tf_op jit(solution)/shard_map/ppermute | solution.py:245
  27.9 7.2 %collective-permute-start.6 = (bf16[64,1536]{1,0:T(8,128)(2,1)S(1)}, bf16[64,1536]{1,0:T(8,128)(2,1)S(1)}, u32[]{:S(2)}, u32[]{:S(2)}) collective-permute-start(bf16[64,1536]{1,0:T(8,128)(2,1)S(1)} %collective-permute-done.4.refs_5_), channel_id=1, source_target_pairs={{0,1},{1,0},{2,3},{3,2},{4,5},{5,4},{6,7},{7,6},{8,9},{9,8},{10,11... | collective-permute-start | bytes 589832 | tf_op jit(solution)/shard_map/ppermute | solution.py:245
  45.6 9.2 %collective-permute-start.15 = (bf16[4,96,384]{2,1,0:T(8,128)(2,1)}, bf16[4,96,384]{2,1,0:T(8,128)(2,1)S(1)}, u32[]{:S(2)}, u32[]{:S(2)}) collective-permute-start(bf16[4,96,384]{2,1,0:T(8,128)(2,1)} %get-tuple-element.37), channel_id=1, source_target_pairs={{0,16},{16,0},{1,17},{17,1},{2,18},{18,2},{3,19},{19,3},{4,20},{20... | collective-permute-start | bytes 884744 | tf_op jit(solution)/shard_map/ppermute | solution.py:245
  51.6 36.1 %collective-permute-start.12 = (bf16[2,2,64,1536]{3,2,1,0:T(8,128)(2,1)}, bf16[2,2,64,1536]{3,2,1,0:T(8,128)(2,1)S(1)}, u32[]{:S(2)}, u32[]{:S(2)}) collective-permute-start(bf16[2,2,64,1536]{3,2,1,0:T(8,128)(2,1)} %get-tuple-element.35), channel_id=1, source_target_pairs={{0,1},{1,0},{2,3},{3,2},{4,5},{5,4},{6,7},{7,6},{8,9},{9,8},{10,11... | collective-permute-start | bytes 2359304 | tf_op jit(solution)/shard_map/ppermute | solution.py:245
  51.7 9.4 %collective-permute-start.22 = (bf16[4,96,384]{2,1,0:T(8,128)(2,1)S(1)}, bf16[4,96,384]{2,1,0:T(8,128)(2,1)S(1)}, u32[]{:S(2)}, u32[]{:S(2)}) collective-permute-start(bf16[4,96,384]{2,1,0:T(8,128)(2,1)S(1)} %copy-done.7), channel_id=1, source_target_pairs={{0,16},{16,0},{1,17},{17,1},{2,18},{18,2},{3,19},{19,3},{4,20},{20... | collective-permute-start | bytes 884744 | tf_op jit(solution)/shard_map/ppermute | solution.py:245
  54.9 6.4 %collective-permute-start.16 = (bf16[4,48,384]{2,1,0:T(8,128)(2,1)S(1)}, bf16[4,48,384]{2,1,0:T(8,128)(2,1)S(1)}, u32[]{:S(2)}, u32[]{:S(2)}) collective-permute-start(bf16[4,48,384]{2,1,0:T(8,128)(2,1)S(1)} %constant_dynamic-slice_fusion.5), channel_id=1, source_target_pairs={{0,4},{4,0},{8,12},{12,8},{1,5},{5,1},{9,13},{13,9},{2,6},{6,2},{1... | collective-permute-start | bytes 442376 | tf_op jit(solution)/shard_map/ppermute | solution.py:245
  61.2 7.0 %collective-permute-start.23 = (bf16[4,48,384]{2,1,0:T(8,128)(2,1)S(1)}, bf16[4,48,384]{2,1,0:T(8,128)(2,1)S(1)}, u32[]{:S(2)}, u32[]{:S(2)}) collective-permute-start(bf16[4,48,384]{2,1,0:T(8,128)(2,1)S(1)} %constant_dynamic-slice_fusion.2), channel_id=1, source_target_pairs={{0,4},{4,0},{8,12},{12,8},{1,5},{5,1},{9,13},{13,9},{2,6},{6,2},{1... | collective-permute-start | bytes 442376 | tf_op jit(solution)/shard_map/ppermute | solution.py:245
  61.4 6.9 %collective-permute-start.17 = (bf16[4,24,384]{2,1,0:T(8,128)(2,1)S(1)}, bf16[4,24,384]{2,1,0:T(8,128)(2,1)S(1)}, u32[]{:S(2)}, u32[]{:S(2)}) collective-permute-start(bf16[4,24,384]{2,1,0:T(8,128)(2,1)S(1)} %constant_dynamic-slice_fusion.4), channel_id=1, source_target_pairs={{0,8},{4,12},{8,0},{12,4},{1,9},{5,13},{9,1},{13,5},{2,10},{6,14},... | collective-permute-start | bytes 221192 | tf_op jit(solution)/shard_map/ppermute | solution.py:245
  77.9 7.6 %collective-permute-start.20 = (bf16[24,1536]{1,0:T(8,128)(2,1)S(1)}, bf16[24,1536]{1,0:T(8,128)(2,1)S(1)}, u32[]{:S(2)}, u32[]{:S(2)}) collective-permute-start(bf16[24,1536]{1,0:T(8,128)(2,1)S(1)} %shard_map.87), channel_id=1, source_target_pairs={{0,8},{4,12},{8,0},{12,4},{1,9},{5,13},{9,1},{13,5},{2,10},{6,14},... | collective-permute-start | bytes 221192 | tf_op jit(solution)/shard_map/ppermute | solution.py:245
  79.1 7.3 %collective-permute-start.27 = (bf16[24,1536]{1,0:T(8,128)(2,1)S(1)}, bf16[24,1536]{1,0:T(8,128)(2,1)S(1)}, u32[]{:S(2)}, u32[]{:S(2)}) collective-permute-start(bf16[24,1536]{1,0:T(8,128)(2,1)S(1)} %shard_map.88), channel_id=1, source_target_pairs={{0,8},{4,12},{8,0},{12,4},{1,9},{5,13},{9,1},{13,5},{2,10},{6,14},... | collective-permute-start | bytes 221192 | tf_op jit(solution)/shard_map/ppermute | solution.py:245
  86.4 6.7 %collective-permute-start.28 = (bf16[48,1536]{1,0:T(8,128)(2,1)S(1)}, bf16[48,1536]{1,0:T(8,128)(2,1)S(1)}, u32[]{:S(2)}, u32[]{:S(2)}) collective-permute-start(bf16[48,1536]{1,0:T(8,128)(2,1)S(1)} %pad_maximum_fusion.4), channel_id=1, source_target_pairs={{0,4},{4,0},{8,12},{12,8},{1,5},{5,1},{9,13},{13,9},{2,6},{6,2},{1... | collective-permute-start | bytes 442376 | tf_op jit(solution)/shard_map/ppermute | solution.py:245
  87.9 12.1 %collective-permute-start.13 = (bf16[1,2,64,1536]{3,2,1,0:T(8,128)(2,1)S(1)}, bf16[1,2,64,1536]{3,2,1,0:T(8,128)(2,1)S(1)}, u32[]{:S(2)}, u32[]{:S(2)}) collective-permute-start(bf16[1,2,64,1536]{3,2,1,0:T(8,128)(2,1)S(1)} %slice.82), channel_id=1, source_target_pairs={{0,2},{1,3},{2,0},{3,1},{4,6},{5,7},{6,4},{7,5},{8,10},{9,11},{10,... | collective-permute-start | bytes 1179656 | tf_op jit(solution)/shard_map/ppermute | solution.py:245
  91.6 8.3 %collective-permute-start.29 = (bf16[96,1536]{1,0:T(8,128)(2,1)S(1)}, bf16[96,1536]{1,0:T(8,128)(2,1)S(1)}, u32[]{:S(2)}, u32[]{:S(2)}) collective-permute-start(bf16[96,1536]{1,0:T(8,128)(2,1)S(1)} %pad_maximum_fusion.1), channel_id=1, source_target_pairs={{0,16},{16,0},{1,17},{17,1},{2,18},{18,2},{3,19},{19,3},{4,20},{20... | collective-permute-start | bytes 884744 | tf_op jit(solution)/shard_map/ppermute | solution.py:245
  93.2 9.9 %collective-permute-start.30 = (bf16[96,1536]{1,0:T(8,128)(2,1)S(1)}, bf16[96,1536]{1,0:T(8,128)(2,1)S(1)}, u32[]{:S(2)}, u32[]{:S(2)}) collective-permute-start(bf16[96,1536]{1,0:T(8,128)(2,1)S(1)} %pad_maximum_fusion.2), channel_id=1, source_target_pairs={{0,16},{16,0},{1,17},{17,1},{2,18},{18,2},{3,19},{19,3},{4,20},{20... | collective-permute-start | bytes 884744 | tf_op jit(solution)/shard_map/ppermute | solution.py:245
  100.2 7.5 %collective-permute-start.14 = (bf16[64,1536]{1,0:T(8,128)(2,1)S(1)}, bf16[64,1536]{1,0:T(8,128)(2,1)S(1)}, u32[]{:S(2)}, u32[]{:S(2)}) collective-permute-start(bf16[64,1536]{1,0:T(8,128)(2,1)S(1)} %get-tuple-element.46), channel_id=1, source_target_pairs={{0,4},{4,8},{8,12},{12,0},{1,5},{5,9},{9,13},{13,1},{2,6},{6,10},{... | collective-permute-start | bytes 589832 | tf_op jit(solution)/shard_map/ppermute | solution.py:19
  (27 other events, 209.3 us)
